TPU v7x, 32 devices: a 4x4x1 block of a 4x4x8 slice. The times are simulated.
32 devices in a mesh: dp: 1 (over z), sp: 32 (over y, x, core).
Axes of the slice: x: 4, y: 4, z: 1, core: 2. Of those that a mesh axis runs over, the one named last changes fastest.
The devices are a block of a 4x4x8 slice.
Arguments:
- hidden: bfloat16 [512, 2048], P(('dp', 'sp'))
- w_q: bfloat16 [2048, 4096], replicated
- w_k: bfloat16 [2048, 512], replicated
- w_v: bfloat16 [2048, 512], replicated
- w_o: bfloat16 [4096, 2048], replicated
- expert_ids: int32 [512, 2], P(('dp', 'sp'))
- router_probs: float32 [512, 128], P(('dp', 'sp'))
Outputs:
- output 1: bfloat16 [512, 2048], P(('dp', 'sp'))
- output 2: bfloat16 [128, 512, 2048], P(('dp', 'sp'))
All inputs are finite; a program needn't handle non-finite values.
Results may differ from a plain program's by a relative error of at most 0.00957174.
Values are sent between devices in bfloat16 or wider.
A program may use at most 768 MiB of HBM per device.

v0:
```python
import math
import jax
import jax.numpy as jnp
from jax import lax
from jax.sharding import PartitionSpec as P

HEAD_DIM = 128
SCORE_SCALE = 1.0 / math.sqrt(HEAD_DIM)


def route_rows(hidden_out, expert_ids, router_probs):
    tok_dev, width = hidden_out.shape
    experts = router_probs.shape[1]
    picked = jnp.take_along_axis(router_probs, expert_ids, axis=1)
    gate_w = picked / jnp.sum(picked, axis=1, keepdims=True)
    gated = (gate_w[:, :, None] * hidden_out[:, None, :].astype(jnp.float32)).astype(jnp.bfloat16)
    token_hits = jnp.sum((expert_ids[:, :, None] == jnp.arange(experts)).astype(jnp.int32), axis=1)
    earlier = jnp.cumsum(token_hits, axis=0) - token_hits
    slot_rank = jnp.take_along_axis(earlier, expert_ids, axis=1)
    send_buf = jnp.zeros((experts, tok_dev, width), jnp.bfloat16)
    return send_buf.at[expert_ids, slot_rank].set(gated, unique_indices=True)


def solution(mesh):
    group = mesh.shape['sp']
    row_spec = P(('dp', 'sp'), None)
    buf_spec = P(('dp', 'sp'), None, None)

    def device_step(x_loc, w_q, w_k, w_v, w_o, ids_loc, probs_loc):
        tok_dev = x_loc.shape[0]
        seq_len = tok_dev * group
        n_heads = w_q.shape[1] // HEAD_DIM
        kv_heads = w_k.shape[1] // HEAD_DIM
        kv_copies = max(1, group // kv_heads)
        head_dev = n_heads // group
        kv_dev = kv_heads * kv_copies // group
        q_loc = jnp.dot(x_loc, w_q, preferred_element_type=jnp.float32).astype(jnp.bfloat16).reshape(tok_dev, n_heads, HEAD_DIM)
        k_loc = jnp.dot(x_loc, w_k, preferred_element_type=jnp.float32).astype(jnp.bfloat16).reshape(tok_dev, kv_heads, HEAD_DIM)
        v_loc = jnp.dot(x_loc, w_v, preferred_element_type=jnp.float32).astype(jnp.bfloat16).reshape(tok_dev, kv_heads, HEAD_DIM)
        k_loc = jnp.repeat(k_loc, kv_copies, axis=1)
        v_loc = jnp.repeat(v_loc, kv_copies, axis=1)
        q_seq = lax.all_to_all(q_loc, 'sp', 1, 0, tiled=True)
        k_seq = lax.all_to_all(k_loc, 'sp', 1, 0, tiled=True)
        v_seq = lax.all_to_all(v_loc, 'sp', 1, 0, tiled=True)
        q_grp = q_seq.reshape(seq_len, kv_dev, head_dev // kv_dev, HEAD_DIM)
        scores = jnp.einsum('qgmd,kgd->gmqk', q_grp, k_seq, preferred_element_type=jnp.float32) * SCORE_SCALE
        positions = jnp.arange(seq_len)
        causal = positions[:, None] >= positions[None, :]
        weights = jax.nn.softmax(jnp.where(causal, scores, -1e30), axis=-1).astype(jnp.bfloat16)
        attn_seq = jnp.einsum('gmqk,kgd->qgmd', weights, v_seq, preferred_element_type=jnp.float32).astype(jnp.bfloat16)
        attn_seq = attn_seq.reshape(seq_len, head_dev, HEAD_DIM)
        attn_loc = lax.all_to_all(attn_seq, 'sp', 0, 1, tiled=True).reshape(tok_dev, n_heads * HEAD_DIM)
        out_proj = jnp.dot(attn_loc, w_o, preferred_element_type=jnp.float32)
        hidden_out = (x_loc.astype(jnp.float32) + out_proj).astype(jnp.bfloat16)
        send_buf = route_rows(hidden_out, ids_loc, probs_loc)
        recv_buf = lax.all_to_all(send_buf, 'sp', 0, 1, tiled=True)
        return hidden_out, recv_buf

    return jax.shard_map(device_step, mesh=mesh, in_specs=(row_spec, P(), P(), P(), P(), row_spec, row_spec), out_specs=(row_spec, buf_spec), check_vma=False)
```

profile of v0, /device:TPU:97, one launch (start us, length us, event | category | flops | bytes accessed | tf_op | source)
XLA Modules:
  0.0 198.7 jit_solution(4816260552110235358)
XLA Ops:
  0.6 0.0 copy-start
  0.6 0.0 copy-start.2
  0.7 0.0 copy-start.3
  0.7 0.0 copy-start.1
  0.7 1.6 copy-done
  2.3 1.2 fusion.6
  3.5 0.7 broadcast_in_dim.37
  4.2 9.1 %all-to-all-start.1 = ((bf16[16,32,128]{2,0,1:T(8,128)(2,1)}), bf16[16,32,128]{2,0,1:T(8,128)(2,1)S(1)}, u32[]{:S(2)}, u32[]{:S(2)}) async-start(bf16[16,32,128]{2,0,1:T(8,128)(2,1)} %bitcast.4), calls=%async_computation.1 | async-start | bytes 262144 | tf_op jit(solution)/shard_map/all_to_all | solution.py:43
  13.3 0.7 fusion.12
  14.0 0.1 copy.86
  14.1 0.1 reshape.113
  14.2 0.0 copy-done.1
  14.2 0.7 gather_fusion.1
  14.9 0.1 reshape.122
  15.0 0.1 copy.89
  15.1 8.1 %fusion.4 = bf16[2,32,8,128]{3,2,1,0:T(8,128)(2,1)S(1)} fusion(bf16[16,2048]{1,0:T(8,128)(2,1)S(1)} %copy-done.2, bf16[2048,4096]{1,0:T(8,128)(2,1)} %param.8), kind=kOutput, calls=%fused_computation.11 | convolution fusion | flops 268500992 | bytes 16973824 | tf_op jit(solution)/shard_map/dot_general | solution.py:37
  23.2 0.1 copy.90
  23.3 0.1 convert_reduce_fusion
  23.4 0.7 gather_fusion
  24.1 0.1 reshape.116
  24.2 0.1 copy.87
  24.2 0.7 copy.106
  24.9 0.0 all-to-all-done.1
  24.9 6.3 %all-to-all-start.2 = ((bf16[16,32,128]{2,0,1:T(8,128)(2,1)}), bf16[16,32,128]{2,0,1:T(8,128)(2,1)S(1)}, u32[]{:S(2)}, u32[]{:S(2)}) async-start(bf16[16,32,128]{2,0,1:T(8,128)(2,1)} %bitcast.80), calls=%async_computation.2 | async-start | bytes 262144 | tf_op jit(solution)/shard_map/all_to_all | solution.py:42
  31.2 2.0 fusion.5
  33.2 5.3 %all-to-all-done.2 = bf16[16,32,128]{2,0,1:T(8,128)(2,1)S(1)} async-done(((bf16[16,32,128]{2,0,1:T(8,128)(2,1)}), bf16[16,32,128]{2,0,1:T(8,128)(2,1)S(1)}, u32[]{:S(2)}, u32[]{:S(2)}) %all-to-all-start.2) | async-done | bytes 131104 | tf_op jit(solution)/shard_map/all_to_all | solution.py:42
  38.5 0.7 broadcast_in_dim.36
  39.1 3.5 %all-to-all-start = ((bf16[16,32,128]{2,0,1:T(8,128)(2,1)}), bf16[16,32,128]{2,0,1:T(8,128)(2,1)}, u32[]{:S(2)}, u32[]{:S(2)}) async-start(bf16[16,32,128]{2,0,1:T(8,128)(2,1)} %bitcast), calls=%async_computation | async-start | bytes 262144 | tf_op jit(solution)/shard_map/all_to_all | solution.py:44
  42.6 0.3 fusion.15
  42.9 0.2 fusion.7
  43.1 7.1 %all-to-all-done = bf16[16,32,128]{2,0,1:T(8,128)(2,1)} async-done(((bf16[16,32,128]{2,0,1:T(8,128)(2,1)}), bf16[16,32,128]{2,0,1:T(8,128)(2,1)}, u32[]{:S(2)}, u32[]{:S(2)}) %all-to-all-start) | async-done | bytes 131104 | tf_op jit(solution)/shard_map/all_to_all | solution.py:44
  50.3 1.2 fusion.3
  51.5 0.5 broadcast.102
  52.0 0.7 reduce.2
  52.7 0.1 copy.109
  52.8 0.7 reshape.131
  53.5 2.9 %all-to-all-start.3 = ((bf16[32,2,1024]{2,1,0:T(2,128)(2,1)}), bf16[32,2,1024]{2,1,0:T(2,128)(2,1)S(1)}, u32[]{:S(2)}, u32[]{:S(2)}) async-start(bf16[32,2,1024]{2,1,0:T(2,128)(2,1)} %reshape.131), calls=%async_computation.3 | async-start | bytes 262144 | tf_op jit(solution)/shard_map/all_to_all | solution.py:52
  56.4 0.1 copy.88
  56.5 0.1 reshape.125
  56.6 7.3 %all-to-all-done.3 = bf16[32,2,1024]{2,1,0:T(2,128)(2,1)S(1)} async-done(((bf16[32,2,1024]{2,1,0:T(2,128)(2,1)}), bf16[32,2,1024]{2,1,0:T(2,128)(2,1)S(1)}, u32[]{:S(2)}, u32[]{:S(2)}) %all-to-all-start.3) | async-done | bytes 131104 | tf_op jit(solution)/shard_map/all_to_all | solution.py:52
  63.9 0.1 reshape.132
  64.1 8.7 %fusion.16 = (f32[16,2048]{1,0:T(8,128)S(1)}, bf16[16,2048]{1,0:T(8,128)(2,1)}) fusion(bf16[4096,2048]{1,0:T(8,128)(2,1)} %param.11, bf16[2,8,32,128]{3,2,1,0:T(8,128)(2,1)S(1)} %bitcast.86, bf16[16,2048]{1,0:T(8,128)(2,1)S(1)} %copy-done.2), kind=kOutput, calls=%fused_computation.43 | convolution fusion | flops 268566528 | bytes 17170432 | tf_op jit(solution)/shard_map/dot_general | solution.py:53
  72.8 0.2 multiply_convert_fusion
  72.9 0.1 reshape.127
  73.0 4.5 %broadcast_in_dim.39 = bf16[128,16,2048]{2,1,0:T(8,128)(2,1)} broadcast(bf16[]{:T(256)} %constant.25.clone.1), dimensions={} | broadcast | bytes 8388610 | tf_op jit(solution)/shard_map/broadcast_in_dim | solution.py:20
  77.5 6.3 %scatter_fusion = bf16[128,16,2048]{2,1,0:T(8,128)(2,1)} fusion(bf16[128,16,2048]{2,1,0:T(8,128)(2,1)} %broadcast_in_dim.39, s32[32]{0:T(128)S(1)} %reshape.125, bf16[32,2048]{1,0:T(8,128)(2,1)S(1)} %reshape.127), kind=kCustom, calls=%fused_computation.2 | custom fusion | bytes 393472 | tf_op jit(solution)/shard_map/scatter | solution.py:21
  83.8 106.4 %all_to_all.78 = bf16[128,16,2048]{2,1,0:T(8,128)(2,1)} all-to-all(bf16[128,16,2048]{2,1,0:T(8,128)(2,1)} %scatter_fusion), channel_id=1, replica_groups=mesh['dp'=1,'sp'=32] {'sp'}, dimensions={0} | all-to-all | bytes 16777216 | tf_op jit(solution)/shard_map/all_to_all | solution.py:56
  190.2 8.4 %copy.91 = bf16[4,32,16,2048]{3,2,1,0:T(8,128)(2,1)} copy(bf16[4,32,16,2048]{3,2,0,1:T(8,128)(2,1)} %bitcast.84) | data formatting | bytes 16777216 | tf_op jit(solution)/shard_map/all_to_all | solution.py:56
  (11 shorter events, 0.2 us)
Async XLA Ops:
  0.6 1.6 copy-start
  0.6 14.4 %copy-start.2 = (bf16[16,2048]{1,0:T(8,128)(2,1)S(1)}, bf16[16,2048]{1,0:T(8,128)(2,1)}, u32[]{:S(2)}) copy-start(bf16[16,2048]{1,0:T(8,128)(2,1)} %param.7) | copy-start | bytes 196612
  0.7 14.4 %copy-start.3 = (s32[16,2]{0,1:T(2,128)S(1)}, s32[16,2]{0,1:T(2,128)}, u32[]{:S(2)}) copy-start(s32[16,2]{0,1:T(2,128)} %param.12) | copy-start | bytes 388
  0.7 13.5 %copy-start.1 = (f32[16,128]{1,0:T(8,128)S(1)}, f32[16,128]{1,0:T(8,128)}, u32[]{:S(2)}) copy-start(f32[16,128]{1,0:T(8,128)} %param.13) | copy-start | bytes 24580
  4.2 20.8 %all-to-all-start.1 = ((bf16[16,32,128]{2,0,1:T(8,128)(2,1)}), bf16[16,32,128]{2,0,1:T(8,128)(2,1)S(1)}, u32[]{:S(2)}, u32[]{:S(2)}) async-start(bf16[16,32,128]{2,0,1:T(8,128)(2,1)} %bitcast.4), calls=%async_computation.1 | async-start | bytes 262144 | tf_op jit(solution)/shard_map/all_to_all | solution.py:43
  24.9 13.5 %all-to-all-start.2 = ((bf16[16,32,128]{2,0,1:T(8,128)(2,1)}), bf16[16,32,128]{2,0,1:T(8,128)(2,1)S(1)}, u32[]{:S(2)}, u32[]{:S(2)}) async-start(bf16[16,32,128]{2,0,1:T(8,128)(2,1)} %bitcast.80), calls=%async_computation.2 | async-start | bytes 262144 | tf_op jit(solution)/shard_map/all_to_all | solution.py:42
  39.1 11.1 %all-to-all-start = ((bf16[16,32,128]{2,0,1:T(8,128)(2,1)}), bf16[16,32,128]{2,0,1:T(8,128)(2,1)}, u32[]{:S(2)}, u32[]{:S(2)}) async-start(bf16[16,32,128]{2,0,1:T(8,128)(2,1)} %bitcast), calls=%async_computation | async-start | bytes 262144 | tf_op jit(solution)/shard_map/all_to_all | solution.py:44
  53.5 10.4 %all-to-all-start.3 = ((bf16[32,2,1024]{2,1,0:T(2,128)(2,1)}), bf16[32,2,1024]{2,1,0:T(2,128)(2,1)S(1)}, u32[]{:S(2)}, u32[]{:S(2)}) async-start(bf16[32,2,1024]{2,1,0:T(2,128)(2,1)} %reshape.131), calls=%async_computation.3 | async-start | bytes 262144 | tf_op jit(solution)/shard_map/all_to_all | solution.py:52
where the time goes:
time: 200 us; the launch traced here: 199 us
  blocking collectives  106 us (53%)
  local copies, waits for them, and re-layouts  26.6 us (13%)
  starting transfers between devices  21.8 us (11%)
  matrix products  21.5 us (11%)
  waiting for transfers between devices  19.7 us (10%)
    all_to_all x1, blocking collectives, device_step(): recv_buf = lax.all_to_all(send_buf, 'sp', 0, 1, tiled=True)  106 us
    all_to_all x1, starting transfers between devices, device_step(): k_seq = lax.all_to_all(k_loc, 'sp', 1, 0, tiled=True)  9.14 us
    dot_general x1, matrix products, device_step(): out_proj = jnp.dot(attn_loc, w_o, preferred_element_type=jnp.float32)  8.7 us
    all_to_all x1, local copies, waits for them, and re-layouts, device_step(): recv_buf = lax.all_to_all(send_buf, 'sp', 0, 1, tiled=True)  8.44 us
    dot_general x1, matrix products, device_step(): jnp.dot(x_loc, w_q, preferred_element_type=jnp.float32).astype(jnp.bfloat16)  8.05 us
    all_to_all x1, waiting for transfers between devices, device_step(): lax.all_to_all(attn_seq, 'sp', 0, 1, tiled=True)  7.3 us
    all_to_all x1, waiting for transfers between devices, device_step(): v_seq = lax.all_to_all(v_loc, 'sp', 1, 0, tiled=True)  7.14 us
    scatter x1, local copies, waits for them, and re-layouts, route_rows(): return send_buf.at[expert_ids, slot_rank].set(gated, unique_indices=True)  6.35 us
  transfers between devices with their start and end apart: 4, of which 3 were waited for; matrix products, arithmetic and copies ran while one was open for 7% of the time, Pallas kernels for 0%

commit v1 on v0

v1 whole, which is shorter than its diff:
```python
import functools
import math

import jax
import jax.numpy as jnp
from jax import lax
from jax.experimental import pallas as pl
from jax.experimental.pallas import tpu as pltpu
from jax.sharding import PartitionSpec as P

HEAD_DIM = 128
SCORE_SCALE = 1.0 / math.sqrt(HEAD_DIM)
MESH_IDS = pl.DeviceIdType.MESH
LANES = 128
CORES = 2
Q_COLS = 512
F32 = jnp.float32
BF16 = jnp.bfloat16


def block_kernel(side, x_hbm, wq_hbm, wk_hbm, wv_hbm, wo_hbm, ids_ref, probs_ref,
                 buf_out, h_out,
                 xbuf, wq_v, wk_v, wv_v, wo_v, kvbuf, meta_own, meta_buf, q_s, o_own, o_sib, h_buf, sel_s, gate_s,
                 wsem, xsem, pair_send, pair_recv, kv_send, kv_recv, mt_send, mt_recv, h_send, h_recv,
                 d_send, d_recv):
    tok = x_hbm.shape[0]
    width = x_hbm.shape[1]
    tok2 = CORES * tok
    half_q = wq_v.shape[1]
    half_kv = wk_v.shape[1]
    half_w = wo_v.shape[1]
    kv_half_heads = half_kv // HEAD_DIM
    q_half_heads = half_q // HEAD_DIM
    per_kv = q_half_heads // kv_half_heads
    own_experts = buf_out.shape[0]
    experts = probs_ref.shape[1]
    n_chips = side * side

    me = lax.axis_index('sp')
    core = me % CORES
    chip = me // CORES
    cy = chip // side
    cx = chip % side
    a0 = cx + (cy - cx) * core
    b0 = cy + (cx - cy) * core

    def chip_of(da, db):
        a = (a0 + (da + side)) % side
        b = (b0 + (db + side)) % side
        y = b + (a - b) * core
        x = a + (b - a) * core
        return y * side + x

    def dev_of(da, db):
        return {'sp': chip_of(da, db) * CORES + core}

    sib = {'sp': chip * CORES + (1 - core)}

    my_rows = pl.ds(pl.multiple_of(core * tok, tok), tok)
    x_load = pltpu.make_async_copy(x_hbm, xbuf.at[my_rows, :], xsem)
    x_load.start()
    loads = {}

    def load(name, src, dst):
        loads[name] = pltpu.make_async_copy(src, dst, wsem.at[len(loads)])
        loads[name].start()

    kv_cols = pl.ds(pl.multiple_of(core * half_kv, half_kv), half_kv)
    load('k', wk_hbm.at[:, kv_cols], wk_v)
    load('v', wv_hbm.at[:, kv_cols], wv_v)
    n_q = half_q // Q_COLS
    for i in range(n_q):
        load(('q', i), wq_hbm.at[:, pl.ds(pl.multiple_of(core * half_q + i * Q_COLS, Q_COLS), Q_COLS)],
             wq_v.at[:, pl.ds(i * Q_COLS, Q_COLS)])
    o_cols = pl.ds(pl.multiple_of(core * half_w, half_w), half_w)
    load('o0', wo_hbm.at[pl.ds(pl.multiple_of(core * half_q, half_q), half_q), o_cols], wo_v.at[pl.ds(0, half_q), :])
    load('o1', wo_hbm.at[pl.ds(pl.multiple_of((1 - core) * half_q, half_q), half_q), o_cols],
         wo_v.at[pl.ds(half_q, half_q), :])

    barrier = pltpu.get_barrier_semaphore()
    partners = [dev_of(1, 0), dev_of(-1, 0), dev_of(0, 1), dev_of(0, -1), sib]
    for p in partners:
        pl.semaphore_signal(barrier, inc=1, device_id=p, device_id_type=MESH_IDS)

    ids = ids_ref[...]
    probs = probs_ref[...]
    lane_e = lax.broadcasted_iota(jnp.int32, (tok, experts), 1)
    p0 = jnp.sum(jnp.where(lane_e == ids[:, 0:1], probs, 0.0), axis=1, keepdims=True)
    p1 = jnp.sum(jnp.where(lane_e == ids[:, 1:2], probs, 0.0), axis=1, keepdims=True)
    psum = p0 + p1
    idf = ids.astype(F32)
    lane_t = lax.broadcasted_iota(jnp.int32, (tok, LANES), 1)
    row_t = lax.broadcasted_iota(jnp.int32, (tok, LANES), 0)
    eye = lane_t == row_t + core * tok

    def to_lanes(col):
        return jnp.sum(jnp.where(eye, col, 0.0), axis=0, keepdims=True)

    meta_rows = [to_lanes(idf[:, 0:1]), to_lanes(idf[:, 1:2]), to_lanes(p0 / psum), to_lanes(p1 / psum)]
    meta_own[0] = jnp.concatenate(meta_rows + [jnp.zeros((4, LANES), F32)], axis=0)

    def remote(src, dst, ss, rs, dev):
        return pltpu.make_async_remote_copy(src_ref=src, dst_ref=dst, send_sem=ss, recv_sem=rs,
                                            device_id=dev, device_id_type=MESH_IDS)

    x_load.wait()
    pl.semaphore_wait(barrier, len(partners))
    x_pair = remote(xbuf.at[my_rows, :], xbuf.at[my_rows, :], pair_send.at[0], pair_recv.at[0], sib)
    x_pair.start()
    m_pair = remote(meta_own.at[0], meta_own.at[1], pair_send.at[1], pair_recv.at[1], sib)
    m_pair.start()

    started = []

    class Gather:
        def __init__(self, items):
            self.items = items
            self.flight = {}

        def start(self, key, n, da, db, to_a, to_b):
            slot = chip_of(da, db)
            dev = dev_of(to_a, to_b)
            self.flight[key] = []
            for ref, ss, rs in self.items:
                c = remote(ref(slot), ref(slot), ss.at[n], rs.at[n], dev)
                c.start()
                self.flight[key].append(c)
                started.append(c)

        def wait(self, key):
            for c in self.flight[key]:
                c.wait_recv()

        def open(self):
            self.start((1, 0), 0, 0, 0, 1, 0)
            self.start((3, 0), 1, 0, 0, -1, 0)
            self.spread(0)

        def spread(self, j):
            self.start((j, 1), 3 + 3 * j, -j, 0, 0, 1)
            self.start((j, 3), 3 + 3 * j + 1, -j, 0, 0, -1)

        def relay(self, j):
            if j % 2 == 0:
                self.start((j, 2), 3 + 3 * j + 2, -j, -1, 0, 1)
            else:
                self.start((j, 2), 3 + 3 * j + 2, -j, -3, 0, -1)

        def steps(self):
            self.wait((1, 0))
            self.start((2, 0), 2, -1, 0, 1, 0)
            self.spread(1)
            yield (1, 0)
            self.wait((3, 0))
            self.spread(3)
            yield (3, 0)
            self.wait((0, 1))
            self.relay(0)
            yield (0, 1)
            self.wait((0, 3))
            yield (0, 3)
            self.wait((2, 0))
            self.spread(2)
            yield (2, 0)
            self.wait((1, 3))
            self.relay(1)
            yield (1, 3)
            self.wait((3, 3))
            self.relay(3)
            yield (3, 3)
            for key in ((1, 1), (3, 1), (0, 2)):
                self.wait(key)
                yield key
            self.wait((2, 1))
            self.relay(2)
            yield (2, 1)
            for key in ((2, 3), (1, 2), (3, 2), (2, 2)):
                self.wait(key)
                yield key

    m_pair.wait_recv()
    meta_buf[chip] = meta_own[0] + meta_own[1]
    x_pair.wait_recv()
    xs = xbuf[...]
    loads['k'].wait()
    kvbuf[chip, :, 0:half_kv] = jnp.dot(xs, wk_v[...], preferred_element_type=F32).astype(BF16)
    loads['v'].wait()
    kvbuf[chip, :, half_kv:2 * half_kv] = jnp.dot(xs, wv_v[...], preferred_element_type=F32).astype(BF16)

    kv = Gather([(lambda s: kvbuf.at[s], kv_send, kv_recv), (lambda s: meta_buf.at[s], mt_send, mt_recv)])
    kv.open()

    for i in range(n_q):
        loads[('q', i)].wait()
        cols = slice(i * Q_COLS, (i + 1) * Q_COLS)
        q_s[:, cols] = jnp.dot(xs, wq_v[:, cols], preferred_element_type=F32).astype(BF16)

    for _ in kv.steps():
        pass

    seq = n_chips * tok2
    q_pos = chip * tok2 + lax.broadcasted_iota(jnp.int32, (per_kv * tok2, seq), 0) % tok2
    k_pos = lax.broadcasted_iota(jnp.int32, (per_kv * tok2, seq), 1)
    causal = k_pos <= q_pos
    o_pairs = []
    for g in range(kv_half_heads):
        kc = slice(g * HEAD_DIM, (g + 1) * HEAD_DIM)
        vc = slice(half_kv + g * HEAD_DIM, half_kv + (g + 1) * HEAD_DIM)
        k_all = kvbuf[:, :, kc].reshape(seq, HEAD_DIM)
        v_all = kvbuf[:, :, vc].reshape(seq, HEAD_DIM)
        q_g = jnp.concatenate([q_s[:, (g * per_kv + h) * HEAD_DIM:(g * per_kv + h + 1) * HEAD_DIM]
                               for h in range(per_kv)], axis=0)
        s = lax.dot_general(q_g, k_all, (((1,), (1,)), ((), ())), preferred_element_type=F32) * SCORE_SCALE
        s = jnp.where(causal, s, -1e30)
        e = jnp.exp(s - jnp.max(s, axis=1, keepdims=True))
        w = (e / jnp.sum(e, axis=1, keepdims=True)).astype(BF16)
        o_g = jnp.dot(w, v_all, preferred_element_type=F32).astype(BF16)
        gw = per_kv * HEAD_DIM
        for h in range(per_kv):
            o_own[:, g * gw + h * HEAD_DIM:g * gw + (h + 1) * HEAD_DIM] = o_g[h * tok2:(h + 1) * tok2, :]
        cols = pl.ds(g * gw, gw)
        c = remote(o_own.at[:, cols], o_sib.at[:, cols], pair_send.at[2 + g], pair_recv.at[2 + g], sib)
        c.start()
        o_pairs.append(c)

    loads['o0'].wait()
    acc = jnp.dot(o_own[...], wo_v[0:half_q, :], preferred_element_type=F32)
    loads['o1'].wait()
    for c in o_pairs:
        c.wait_recv()
    acc = acc + jnp.dot(o_sib[...], wo_v[half_q:2 * half_q, :], preferred_element_type=F32)
    my_cols = pl.ds(pl.multiple_of(core * half_w, half_w), half_w)
    h_buf[core, chip] = (xbuf[:, my_cols].astype(F32) + acc).astype(BF16)

    hg = Gather([(lambda s: h_buf.at[core, s], h_send, h_recv)])
    across = {}

    def cross(n, da, db):
        slot = chip_of(da, db)
        c = remote(h_buf.at[core, slot], h_buf.at[core, slot], d_send.at[n], d_recv.at[n], sib)
        c.start()
        across[n] = c
        started.append(c)

    cross(0, 0, 0)
    hg.open()

    lane_1 = lax.broadcasted_iota(jnp.int32, (1, LANES), 1)
    t_row = lax.broadcasted_iota(jnp.int32, (LANES, LANES), 0)
    t_col = lax.broadcasted_iota(jnp.int32, (LANES, LANES), 1)
    before = jnp.where((t_row < t_col) & (t_row // tok == t_col // tok), 1.0, 0.0).astype(BF16)
    source_base = ((lane_1 // tok) * tok).astype(F32)
    live = lane_1 < tok2
    slot_row = lax.broadcasted_iota(jnp.int32, (tok2, LANES), 0).astype(F32)

    def select_rows(s, carry):
        m = meta_buf[s]
        e_first, e_second = m[0:1, :], m[1:2, :]
        sels, gates = [], []
        for k in range(own_experts):
            expert = (me * own_experts + k).astype(F32)
            hit0 = (e_first == expert) & live
            hit1 = (e_second == expert) & live
            hit = jnp.where(hit0 | hit1, 1.0, 0.0)
            slot = jnp.dot(jnp.broadcast_to(hit, (8, LANES)).astype(BF16), before, preferred_element_type=F32)[0:1, :]
            row = jnp.where(hit0 | hit1, slot + source_base, -1.0)
            gate = jnp.where(hit0, m[2:3, :], jnp.where(hit1, m[3:4, :], 0.0))
            pick = slot_row == row
            sels.append(jnp.where(pick, 1.0, 0.0))
            gates.append(jnp.broadcast_to(jnp.sum(jnp.where(pick, gate, 0.0), axis=1, keepdims=True), (tok2, LANES)))
        sel_s[s] = jnp.concatenate(sels, axis=0).astype(BF16)
        gate_s[s] = jnp.concatenate(gates, axis=0)
        return carry

    lax.fori_loop(0, n_chips, select_rows, 0)

    def build(slot, col_half):
        sel = sel_s[slot][:, 0:tok2]
        rows = jnp.dot(sel, h_buf[col_half, slot], preferred_element_type=F32)
        gate = gate_s[slot]
        rows = jnp.concatenate([rows[:, i * LANES:(i + 1) * LANES] * gate for i in range(half_w // LANES)], axis=1)
        rows = rows.astype(BF16)
        at = pl.ds(pl.multiple_of(slot * tok2, tok2), tok2)
        cols = pl.ds(pl.multiple_of(col_half * half_w, half_w), half_w)
        for k in range(own_experts):
            buf_out[k, at, cols] = rows[k * tok2:(k + 1) * tok2, :]

    build(chip, core)
    arrived = [(0, 0)]
    for n, key in enumerate(hg.steps()):
        j, d = key
        cross(n + 1, -j, -d)
        build(chip_of(-j, -d), core)
        arrived.append(key)
    for n, (j, d) in enumerate(arrived):
        across[n].wait_recv()
        build(chip_of(-d, -j), 1 - core)
    h_out[:, 0:half_w] = h_buf[0, chip, my_rows, :]
    h_out[:, half_w:2 * half_w] = h_buf[1, chip, my_rows, :]

    for c in [x_pair, m_pair] + o_pairs + started:
        c.wait_send()


def store_kernel(buf_ref, h_ref, buf_out, h_out, sem):
    n = buf_ref.shape[0]
    copies = [pltpu.make_async_copy(buf_ref.at[k], buf_out.at[k], sem.at[k]) for k in range(n)]
    copies.append(pltpu.make_async_copy(h_ref, h_out, sem.at[n]))
    for c in copies:
        c.start()
    for c in copies:
        c.wait()


def solution(mesh):
    group = mesh.shape['sp']
    side = math.isqrt(group // CORES)
    row_spec = P(('dp', 'sp'), None)
    buf_spec = P(('dp', 'sp'), None, None)
    any_spec = pl.BlockSpec(memory_space=pl.ANY)
    vmem_spec = pl.BlockSpec(memory_space=pltpu.VMEM)

    def device_step(x_loc, w_q, w_k, w_v, w_o, ids_loc, probs_loc):
        tok, width = x_loc.shape
        experts = probs_loc.shape[1]
        own = experts // group
        chips = side * side
        tok2 = CORES * tok
        half_q = w_q.shape[1] // CORES
        half_kv = w_k.shape[1] // CORES
        half_w = width // CORES
        dma = pltpu.SemaphoreType.DMA
        n_loads = 4 + half_q // Q_COLS
        kv_half_heads = half_kv // HEAD_DIM
        buf, h = pl.pallas_call(
            functools.partial(block_kernel, side),
            out_shape=(pltpu.VMEM((own, tok * group, width), BF16), pltpu.VMEM((tok, width), BF16)),
            in_specs=[any_spec] * 5 + [vmem_spec] * 2,
            out_specs=(vmem_spec, vmem_spec),
            scratch_shapes=[
                pltpu.VMEM((tok2, width), BF16),
                pltpu.VMEM((width, half_q), BF16),
                pltpu.VMEM((width, half_kv), BF16),
                pltpu.VMEM((width, half_kv), BF16),
                pltpu.VMEM((2 * half_q, half_w), BF16),
                pltpu.VMEM((chips, tok2, 2 * half_kv), BF16),
                pltpu.VMEM((CORES, 8, LANES), F32),
                pltpu.VMEM((chips, 8, LANES), F32),
                pltpu.VMEM((tok2, half_q), BF16),
                pltpu.VMEM((tok2, half_q), BF16),
                pltpu.VMEM((tok2, half_q), BF16),
                pltpu.VMEM((CORES, chips, tok2, half_w), BF16),
                pltpu.VMEM((chips, own * tok2, LANES), BF16),
                pltpu.VMEM((chips, own * tok2, LANES), F32),
                dma((n_loads,)), dma,
                dma((2 + kv_half_heads,)), dma((2 + kv_half_heads,)),
                dma((chips,)), dma((chips,)), dma((chips,)), dma((chips,)),
                dma((chips,)), dma((chips,)), dma((chips,)), dma((chips,)),
            ],
            compiler_params=pltpu.CompilerParams(collective_id=0, has_side_effects=True,
                                                 vmem_limit_bytes=44 * 2 ** 20),
            name='attention_block',
        )(x_loc, w_q, w_k, w_v, w_o, ids_loc, probs_loc)
        buf, h = pl.pallas_call(
            store_kernel,
            out_shape=(jax.ShapeDtypeStruct((own, tok * group, width), BF16), jax.ShapeDtypeStruct((tok, width), BF16)),
            in_specs=[vmem_spec, vmem_spec],
            out_specs=(any_spec, any_spec),
            scratch_shapes=[dma((own + 1,))],
            compiler_params=pltpu.CompilerParams(vmem_limit_bytes=16 * 2 ** 20),
            name='store_outputs',
        )(buf, h)
        return h, buf

    return jax.shard_map(device_step, mesh=mesh, in_specs=(row_spec, P(), P(), P(), P(), row_spec, row_spec), out_specs=(row_spec, buf_spec), check_vma=False)
```

time: 200 us -> 48.6 us (0.24)
  blocking collectives: 106 us -> 0 us
  Pallas kernels: 0 us -> 45.2 us
  local copies, waits for them, and re-layouts: 26.6 us -> 2.29 us
  starting transfers between devices: 21.8 us -> 0 us
  matrix products: 21.5 us -> 0 us
  waiting for transfers between devices: 19.7 us -> 0 us
    all_to_all x1 -> x0, blocking collectives: 106 us -> none  [device_step(): recv_buf = lax.all_to_all(send_buf, 'sp', 0, 1, tiled=True)]
    pallas_call x0 -> x2, Pallas kernels: none -> 45.2 us  [the longest x1 41.8 us: device_step(): pl.pallas_call(functools.partial(block_kernel, side), out_shape=(pltpu.VM...]
    all_to_all x4 -> x0, starting transfers between devices: 21.8 us -> none  [the longest x1 9.14 us: device_step(): k_seq = lax.all_to_all(k_loc, 'sp', 1, 0, tiled=True)]
    dot_general x6 -> x0, matrix products: 21.5 us -> none  [the longest x1 8.7 us: device_step(): out_proj = jnp.dot(attn_loc, w_o, preferred_element_type=jnp.float32)]
    all_to_all x4 -> x0, waiting for transfers between devices: 19.7 us -> none  [the longest x1 7.3 us: device_step(): lax.all_to_all(attn_seq, 'sp', 0, 1, tiled=True)]
    all_to_all x2 -> x0, local copies, waits for them, and re-layouts: 8.48 us -> none  [the longest x1 8.44 us: device_step(): recv_buf = lax.all_to_all(send_buf, 'sp', 0, 1, tiled=True)]
    scatter x1 -> x0, local copies, waits for them, and re-layouts: 6.35 us -> none  [route_rows(): return send_buf.at[expert_ids, slot_rank].set(gated, unique_indices=True)]
    broadcast_in_dim x3 -> x0, local copies, waits for them, and re-layouts: 5.82 us -> none  [the longest x1 4.46 us: route_rows(): send_buf = jnp.zeros((experts, tok_dev, width), jnp.bfloat16)]
  transfers between devices with their start and end apart: 4 -> 0, of which waited for: 3 -> 0; matrix products, arithmetic and copies ran while one was open for 7% -> 0% of each run, Pallas kernels for 0% -> 0%
where the time goes in v1:
time: 48.6 us; the launch traced here: 48.1 us
  Pallas kernels  45.2 us (93%)
  local copies, waits for them, and re-layouts  2.29 us (5%)
  between operations  0.64 us (1%)
    pallas_call x1, Pallas kernels, device_step(): pl.pallas_call(functools.partial(block_kernel, side), out_shape=(pltpu.VM...  41.8 us
    pallas_call x1, Pallas kernels, device_step(): pl.pallas_call(store_kernel, out_shape=(jax.ShapeDtypeStruct((own, tok *...  3.38 us
    unnamed x5, local copies, waits for them, and re-layouts  2.29 us

profile of v1, /device:TPU:97, one launch (start us, length us, event | category | flops | bytes accessed | tf_op | source)
XLA Modules:
  0.0 48.1 jit_solution(7056436018752793488)
XLA Ops:
  0.6 0.8 %copy.9.ids_ref = s32[16,2]{1,0:T(8,128)S(1)} copy(s32[16,2]{0,1:T(2,128)} %param.12) | data formatting | bytes 256 | tf_op args[5]
  1.4 0.0 copy-start
  1.4 0.8 %copy-done = bf16[16,2048]{1,0:T(8,128)(2,1)S(1)} copy-done((bf16[16,2048]{1,0:T(8,128)(2,1)S(1)}, bf16[16,2048]{1,0:T(8,128)(2,1)}, u32[]{:S(2)}) %copy-start) | copy-done | bytes 65560
  2.2 0.0 copy-start.1
  2.2 0.7 %copy-done.1 = f32[16,128]{1,0:T(8,128)S(1)} copy-done((f32[16,128]{1,0:T(8,128)S(1)}, f32[16,128]{1,0:T(8,128)}, u32[]{:S(2)}) %copy-start.1) | copy-done | bytes 8216
  2.9 41.8 %attention_block.1 = (bf16[4,512,2048]{2,1,0:T(8,128)(2,1)S(1)}, bf16[16,2048]{1,0:T(8,128)(2,1)S(1)}) custom-call(bf16[16,2048]{1,0:T(8,128)(2,1)S(1)} %copy-done, bf16[2048,4096]{1,0:T(8,128)(2,1)} %wq_hbm.1, bf16[2048,512]{1,0:T(8,128)(2,1)} %wk_hbm.1, bf16[2048,512]{1,0:T(8,128)(2,1)} %wv_hbm.1, bf16[4096,2048]{1,0:T(8,128)(2,1)} %wo_hbm.1, ...), custom_call_target="tpu_custom_call" | custom-call | tf_op jit(solution)/shard_map/attention_block/pallas_call | solution.py:335
  44.7 3.4 %store_outputs.1 = (bf16[4,512,2048]{2,1,0:T(8,128)(2,1)}, bf16[16,2048]{1,0:T(8,128)(2,1)}) custom-call(bf16[4,512,2048]{2,1,0:T(8,128)(2,1)S(1)} %get-tuple-element.6.buf_ref, bf16[16,2048]{1,0:T(8,128)(2,1)S(1)} %get-tuple-element.7.h_ref), custom_call_target="tpu_custom_call" | custom-call | tf_op jit(solution)/shard_map/store_outputs/pallas_call | solution.py:364
Async XLA Ops:
  1.4 0.8 %copy-start = (bf16[16,2048]{1,0:T(8,128)(2,1)S(1)}, bf16[16,2048]{1,0:T(8,128)(2,1)}, u32[]{:S(2)}) copy-start(bf16[16,2048]{1,0:T(8,128)(2,1)} %x_hbm.1) | copy-start | bytes 196612
  2.2 0.7 %copy-start.1 = (f32[16,128]{1,0:T(8,128)S(1)}, f32[16,128]{1,0:T(8,128)}, u32[]{:S(2)}) copy-start(f32[16,128]{1,0:T(8,128)} %probs_ref.1) | copy-start | bytes 24580

commit v2 on v1

v2 whole, which is shorter than its diff:
```python
import functools
import math

import jax
import jax.numpy as jnp
from jax import lax
from jax.experimental import pallas as pl
from jax.experimental.pallas import tpu as pltpu
from jax.sharding import PartitionSpec as P

HEAD_DIM = 128
SCORE_SCALE = 1.0 / math.sqrt(HEAD_DIM)
MESH_IDS = pl.DeviceIdType.MESH
LANES = 128
CORES = 2
Q_COLS = 512
F32 = jnp.float32
BF16 = jnp.bfloat16


def block_kernel(side, x_hbm, wq_hbm, wk_hbm, wv_hbm, wo_hbm, ids_hbm, probs_hbm,
                 buf_out, h_out,
                 xbuf, wq_v, wk_v, wv_v, wo_v, ids_v, probs_v, kv_own, kvbuf, meta_own, meta_buf, q_s, o_own, o_sib,
                 h_buf, sel_s, gate_s,
                 wsem, pair_send, pair_recv, kv_send, kv_recv, mt_send, mt_recv, h_send, h_recv,
                 d_send, d_recv):
    tok = x_hbm.shape[0]
    tok2 = CORES * tok
    half_q = wq_v.shape[1]
    half_kv = wk_v.shape[1] // CORES
    half_w = wo_v.shape[1]
    kv_half_heads = half_kv // HEAD_DIM
    q_half_heads = half_q // HEAD_DIM
    per_kv = q_half_heads // kv_half_heads
    own_experts = buf_out.shape[0]
    experts = probs_v.shape[1]
    n_chips = side * side
    n_dev = n_chips * CORES

    me = lax.axis_index('sp')
    core = me % CORES
    chip = me // CORES
    cy = chip // side
    cx = chip % side
    a0 = cx + (cy - cx) * core
    b0 = cy + (cx - cy) * core

    def chip_at(a, b):
        y = b + (a - b) * core
        x = a + (b - a) * core
        return y * side + x

    def peer(c):
        return {'sp': c * CORES + core}

    sib = {'sp': chip * CORES + (1 - core)}

    def remote(src, dst, ss, rs, dev):
        return pltpu.make_async_remote_copy(src_ref=src, dst_ref=dst, send_sem=ss, recv_sem=rs,
                                            device_id=dev, device_id_type=MESH_IDS)

    my_rows = pl.ds(pl.multiple_of(core * tok, tok), tok)
    loads = {}

    def load(name, src, dst):
        loads[name] = pltpu.make_async_copy(src, dst, wsem.at[len(loads)])
        loads[name].start()

    load('x', x_hbm, xbuf.at[my_rows, :])
    load('ids', ids_hbm, ids_v)
    load('probs', probs_hbm, probs_v)
    load('k', wk_hbm, wk_v)
    load('v', wv_hbm, wv_v)
    n_q = half_q // Q_COLS
    for i in range(n_q):
        load(('q', i), wq_hbm.at[:, pl.ds(pl.multiple_of(core * half_q + i * Q_COLS, Q_COLS), Q_COLS)],
             wq_v.at[:, pl.ds(i * Q_COLS, Q_COLS)])
    o_cols = pl.ds(pl.multiple_of(core * half_w, half_w), half_w)
    load('o0', wo_hbm.at[pl.ds(pl.multiple_of(core * half_q, half_q), half_q), o_cols], wo_v.at[pl.ds(0, half_q), :])
    load('o1', wo_hbm.at[pl.ds(pl.multiple_of((1 - core) * half_q, half_q), half_q), o_cols],
         wo_v.at[pl.ds(half_q, half_q), :])

    kvbuf[...] = jnp.zeros_like(kvbuf)

    barrier = pltpu.get_barrier_semaphore()
    for i in range(1, n_dev):
        pl.semaphore_signal(barrier, inc=1, device_id={'sp': (me + i) % n_dev}, device_id_type=MESH_IDS)

    loads['x'].wait()
    loads['ids'].wait()
    loads['probs'].wait()
    idf = ids_v[...].astype(F32)
    probs = probs_v[...]
    lane_e = lax.broadcasted_iota(jnp.int32, (tok, experts), 1).astype(F32)
    eye_t = lax.broadcasted_iota(jnp.int32, (tok, tok), 0) == lax.broadcasted_iota(jnp.int32, (tok, tok), 1)
    id0 = jnp.sum(jnp.where(eye_t, idf[0:1, :], 0.0), axis=1, keepdims=True)
    id1 = jnp.sum(jnp.where(eye_t, idf[1:2, :], 0.0), axis=1, keepdims=True)
    p0 = jnp.sum(jnp.where(lane_e == id0, probs, 0.0), axis=1, keepdims=True)
    p1 = jnp.sum(jnp.where(lane_e == id1, probs, 0.0), axis=1, keepdims=True)
    psum = p0 + p1
    lane_t = lax.broadcasted_iota(jnp.int32, (tok, LANES), 1)
    row_t = lax.broadcasted_iota(jnp.int32, (tok, LANES), 0)
    eye = lane_t == row_t + core * tok

    def to_lanes(col):
        return jnp.sum(jnp.where(eye, col, 0.0), axis=0, keepdims=True)

    meta_rows = [to_lanes(id0), to_lanes(id1), to_lanes(p0 / psum), to_lanes(p1 / psum)]
    meta_own[0] = jnp.concatenate(meta_rows + [jnp.zeros((4, LANES), F32)], axis=0)

    x_own = xbuf[my_rows, :]
    for name, w_ref, at in (('k', wk_v, 0), ('v', wv_v, half_kv)):
        loads[name].wait()
        out = jnp.dot(x_own, w_ref[...], preferred_element_type=F32).astype(BF16)
        for c in range(CORES):
            kv_own[c, :, at:at + half_kv] = out[:, c * half_kv:(c + 1) * half_kv]
    kvbuf[chip, my_rows, :] = kv_own[core]

    pl.semaphore_wait(barrier, n_dev - 1)
    x_pair = remote(xbuf.at[my_rows, :], xbuf.at[my_rows, :], pair_send.at[0], pair_recv.at[0], sib)
    x_pair.start()
    m_pair = remote(meta_own.at[0], meta_own.at[1], pair_send.at[1], pair_recv.at[1], sib)
    m_pair.start()
    kv_pair = remote(kv_own.at[1 - core], kvbuf.at[chip, my_rows, :], pair_send.at[2], pair_recv.at[2], sib)
    kv_pair.start()

    def kv_copy(k, c, slot, rows, src_core):
        return remote(kv_own.at[c], kvbuf.at[slot, rows, :], kv_send.at[CORES * k + c],
                      kv_recv.at[CORES * k + src_core], {'sp': (chip + k) % n_chips * CORES + c})

    for k in range(1, n_chips):
        @pl.when(chip + k < n_chips)
        def _():
            for c in range(CORES):
                kv_copy(k, c, chip, my_rows, core).start()

    class Gather:
        def __init__(self, ref, ss, rs):
            self.ref, self.ss, self.rs = ref, ss, rs

        def first(self, d, slot):
            return remote(self.ref(slot), self.ref(slot), self.ss.at[d], self.rs.at[a0],
                          peer(chip_at((a0 + d) % side, b0)))

        def first_from(self, i, slot):
            return remote(self.ref(slot), self.ref(slot), self.ss.at[0], self.rs.at[i], sib)

        def second(self, i, d, slot):
            return remote(self.ref(slot), self.ref(slot), self.ss.at[side + i * side + d],
                          self.rs.at[side + i * side + b0], peer(chip_at(a0, (b0 + d) % side)))

        def second_from(self, i, j, slot):
            return remote(self.ref(slot), self.ref(slot), self.ss.at[0], self.rs.at[side + i * side + j], sib)

        def open(self):
            for d in (1, side - 1, 2):
                self.first(d, chip).start()
            self.spread(a0)

        def spread(self, i):
            for d in (1, side - 1, 2):
                self.second(i, d, chip_at(i, b0)).start()

        def sent(self):
            for d in range(1, side):
                self.first(d, chip).wait_send()
                for i in range(side):
                    self.second(i, d, chip_at(i, b0)).wait_send()

    x_pair.wait_recv()
    xs = xbuf[...]
    for i in range(n_q):
        loads[('q', i)].wait()
        cols = slice(i * Q_COLS, (i + 1) * Q_COLS)
        q_s[:, cols] = jnp.dot(xs, wq_v[:, cols], preferred_element_type=F32).astype(BF16)

    m_pair.wait_recv()
    meta_buf[chip] = meta_own[0] + meta_own[1]
    mt = Gather(lambda s: meta_buf.at[s], mt_send, mt_recv)
    mt.open()

    kv_pair.wait_recv()
    for k in range(1, n_chips):
        @pl.when(chip >= k)
        def _():
            for c in range(CORES):
                kv_copy(k, c, chip - k, pl.ds(c * tok, tok), c).wait_recv()

    seq = n_chips * tok2
    q_pos = chip * tok2 + lax.broadcasted_iota(jnp.int32, (per_kv * tok2, seq), 0) % tok2
    k_pos = lax.broadcasted_iota(jnp.int32, (per_kv * tok2, seq), 1)
    causal = k_pos <= q_pos
    o_pairs = []
    for g in range(kv_half_heads):
        kc = slice(g * HEAD_DIM, (g + 1) * HEAD_DIM)
        vc = slice(half_kv + g * HEAD_DIM, half_kv + (g + 1) * HEAD_DIM)
        k_all = kvbuf[:, :, kc].reshape(seq, HEAD_DIM)
        v_all = kvbuf[:, :, vc].reshape(seq, HEAD_DIM)
        q_g = jnp.concatenate([q_s[:, (g * per_kv + h) * HEAD_DIM:(g * per_kv + h + 1) * HEAD_DIM]
                               for h in range(per_kv)], axis=0)
        s = lax.dot_general(q_g, k_all, (((1,), (1,)), ((), ())), preferred_element_type=F32) * SCORE_SCALE
        s = jnp.where(causal, s, -1e30)
        e = jnp.exp(s - jnp.max(s, axis=1, keepdims=True))
        w = (e / jnp.sum(e, axis=1, keepdims=True)).astype(BF16)
        o_g = jnp.dot(w, v_all, preferred_element_type=F32).astype(BF16)
        gw = per_kv * HEAD_DIM
        for h in range(per_kv):
            o_own[:, g * gw + h * HEAD_DIM:g * gw + (h + 1) * HEAD_DIM] = o_g[h * tok2:(h + 1) * tok2, :]
        cols = pl.ds(g * gw, gw)
        c = remote(o_own.at[:, cols], o_sib.at[:, cols], pair_send.at[3 + g], pair_recv.at[3 + g], sib)
        c.start()
        o_pairs.append(c)

    def pass_meta(i, carry):
        @pl.when(i != a0)
        def _():
            mt.first_from(i, chip_at(i, b0)).wait_recv()
            mt.spread(i)
        return carry

    lax.fori_loop(0, side, pass_meta, 0)

    loads['o0'].wait()
    acc = jnp.dot(o_own[...], wo_v[0:half_q, :], preferred_element_type=F32)
    loads['o1'].wait()
    for c in o_pairs:
        c.wait_recv()
    acc = acc + jnp.dot(o_sib[...], wo_v[half_q:2 * half_q, :], preferred_element_type=F32)
    my_cols = pl.ds(pl.multiple_of(core * half_w, half_w), half_w)
    h_buf[core, chip] = (xbuf[:, my_cols].astype(F32) + acc).astype(BF16)

    hg = Gather(lambda s: h_buf.at[core, s], h_send, h_recv)

    def cross(slot):
        return remote(h_buf.at[core, slot], h_buf.at[core, slot], d_send.at[slot], d_recv.at[slot], sib)

    def cross_from(slot):
        return remote(h_buf.at[1 - core, slot], h_buf.at[1 - core, slot], d_send.at[slot], d_recv.at[slot], sib)

    hg.open()
    cross(chip).start()

    def meta_done(n, carry):
        i, j = n // side, n % side

        @pl.when(j != b0)
        def _():
            mt.second_from(i, j, chip_at(i, j)).wait_recv()
        return carry

    lax.fori_loop(0, n_chips, meta_done, 0)

    lane_1 = lax.broadcasted_iota(jnp.int32, (1, LANES), 1)
    t_row = lax.broadcasted_iota(jnp.int32, (LANES, LANES), 0)
    t_col = lax.broadcasted_iota(jnp.int32, (LANES, LANES), 1)
    before = jnp.where((t_row < t_col) & (t_row // tok == t_col // tok), 1.0, 0.0).astype(BF16)
    source_base = ((lane_1 // tok) * tok).astype(F32)
    live = lane_1 < tok2
    slot_row = lax.broadcasted_iota(jnp.int32, (tok2, LANES), 0).astype(F32)

    def select_rows(s, carry):
        m = meta_buf[s]
        e_first, e_second = m[0:1, :], m[1:2, :]
        sels, gates = [], []
        for k in range(own_experts):
            expert = (me * own_experts + k).astype(F32)
            hit0 = (e_first == expert) & live
            hit1 = (e_second == expert) & live
            hit = jnp.where(hit0 | hit1, 1.0, 0.0)
            slot = jnp.dot(jnp.broadcast_to(hit, (8, LANES)).astype(BF16), before, preferred_element_type=F32)[0:1, :]
            row = jnp.where(hit0 | hit1, slot + source_base, -1.0)
            gate = jnp.where(hit0, m[2:3, :], jnp.where(hit1, m[3:4, :], 0.0))
            pick = slot_row == row
            sels.append(jnp.where(pick, 1.0, 0.0))
            gates.append(jnp.broadcast_to(jnp.sum(jnp.where(pick, gate, 0.0), axis=1, keepdims=True), (tok2, LANES)))
        sel_s[s] = jnp.concatenate(sels, axis=0).astype(BF16)
        gate_s[s] = jnp.concatenate(gates, axis=0)
        return carry

    lax.fori_loop(0, n_chips, select_rows, 0)

    def build(slot, col_half):
        sel = sel_s[slot][:, 0:tok2]
        rows = jnp.dot(sel, h_buf[col_half, slot], preferred_element_type=F32)
        gate = gate_s[slot]
        rows = jnp.concatenate([rows[:, i * LANES:(i + 1) * LANES] * gate for i in range(half_w // LANES)], axis=1)
        rows = rows.astype(BF16)
        at = pl.ds(pl.multiple_of(slot * tok2, tok2), tok2)
        cols = pl.ds(pl.multiple_of(col_half * half_w, half_w), half_w)
        for k in range(own_experts):
            buf_out[k, at, cols] = rows[k * tok2:(k + 1) * tok2, :]

    build(chip, core)

    def pass_first(i, carry):
        @pl.when(i != a0)
        def _():
            slot = chip_at(i, b0)
            hg.first_from(i, slot).wait_recv()
            hg.spread(i)
            cross(slot).start()
            build(slot, core)
        return carry

    lax.fori_loop(0, side, pass_first, 0)

    lag = side

    def pass_second(slot, carry):
        y, x = slot // side, slot % side
        i = x + (y - x) * core
        j = y + (x - y) * core

        @pl.when((slot < n_chips) & (j != b0))
        def _():
            hg.second_from(i, j, slot).wait_recv()
            cross(slot).start()
            build(slot, core)

        @pl.when(slot >= lag)
        def _():
            cross_from(slot - lag).wait_recv()
            build(slot - lag, 1 - core)
        return carry

    lax.fori_loop(0, n_chips + lag, pass_second, 0)
    h_out[:, 0:half_w] = h_buf[0, chip, my_rows, :]
    h_out[:, half_w:2 * half_w] = h_buf[1, chip, my_rows, :]

    for c in [x_pair, m_pair, kv_pair] + o_pairs:
        c.wait_send()
    for k in range(1, n_chips):
        @pl.when(chip + k < n_chips)
        def _():
            for c in range(CORES):
                kv_copy(k, c, chip, my_rows, core).wait_send()
    mt.sent()
    hg.sent()
    for slot in range(n_chips):
        cross(slot).wait_send()


def store_kernel(buf_ref, h_ref, buf_out, h_out, sem):
    n = buf_ref.shape[0]
    copies = [pltpu.make_async_copy(buf_ref.at[k], buf_out.at[k], sem.at[k]) for k in range(n)]
    copies.append(pltpu.make_async_copy(h_ref, h_out, sem.at[n]))
    for c in copies:
        c.start()
    for c in copies:
        c.wait()


def solution(mesh):
    group = mesh.shape['sp']
    side = math.isqrt(group // CORES)
    row_spec = P(('dp', 'sp'), None)
    buf_spec = P(('dp', 'sp'), None, None)
    any_spec = pl.BlockSpec(memory_space=pl.ANY)
    hbm_spec = pl.BlockSpec(memory_space=pltpu.HBM)
    vmem_spec = pl.BlockSpec(memory_space=pltpu.VMEM)

    def device_step(x_loc, w_q, w_k, w_v, w_o, ids_loc, probs_loc):
        tok, width = x_loc.shape
        experts = probs_loc.shape[1]
        own = experts // group
        chips = side * side
        tok2 = CORES * tok
        half_q = w_q.shape[1] // CORES
        half_kv = w_k.shape[1] // CORES
        half_w = width // CORES
        dma = pltpu.SemaphoreType.DMA
        n_loads = 7 + half_q // Q_COLS
        kv_half_heads = half_kv // HEAD_DIM
        buf, h = pl.pallas_call(
            functools.partial(block_kernel, side),
            out_shape=(pltpu.VMEM((own, tok * group, width), BF16), pltpu.VMEM((tok, width), BF16)),
            in_specs=[hbm_spec] * 7,
            out_specs=(vmem_spec, vmem_spec),
            scratch_shapes=[
                pltpu.VMEM((tok2, width), BF16),
                pltpu.VMEM((width, half_q), BF16),
                pltpu.VMEM((width, CORES * half_kv), BF16),
                pltpu.VMEM((width, CORES * half_kv), BF16),
                pltpu.VMEM((2 * half_q, half_w), BF16),
                pltpu.VMEM((2, tok), jnp.int32),
                pltpu.VMEM((tok, experts), F32),
                pltpu.VMEM((CORES, tok, 2 * half_kv), BF16),
                pltpu.VMEM((chips, tok2, 2 * half_kv), BF16),
                pltpu.VMEM((CORES, 8, LANES), F32),
                pltpu.VMEM((chips, 8, LANES), F32),
                pltpu.VMEM((tok2, half_q), BF16),
                pltpu.VMEM((tok2, half_q), BF16),
                pltpu.VMEM((tok2, half_q), BF16),
                pltpu.VMEM((CORES, chips, tok2, half_w), BF16),
                pltpu.VMEM((chips, own * tok2, LANES), BF16),
                pltpu.VMEM((chips, own * tok2, LANES), F32),
                dma((n_loads,)),
                dma((3 + kv_half_heads,)), dma((3 + kv_half_heads,)),
                dma((group,)), dma((group,)),
                dma((side + chips,)), dma((side + chips,)), dma((side + chips,)), dma((side + chips,)),
                dma((chips,)), dma((chips,)),
            ],
            compiler_params=pltpu.CompilerParams(collective_id=0, has_side_effects=True,
                                                 vmem_limit_bytes=55 * 2 ** 20 + 850 * 1024),
            name='attention_block',
        )(x_loc, w_q, w_k, w_v, w_o, ids_loc.T, probs_loc)
        buf, h = pl.pallas_call(
            store_kernel,
            out_shape=(jax.ShapeDtypeStruct((own, tok * group, width), BF16), jax.ShapeDtypeStruct((tok, width), BF16)),
            in_specs=[vmem_spec, vmem_spec],
            out_specs=(any_spec, any_spec),
            scratch_shapes=[dma((own + 1,))],
            compiler_params=pltpu.CompilerParams(vmem_limit_bytes=16 * 2 ** 20),
            name='store_outputs',
        )(buf, h)
        return h, buf

    return jax.shard_map(device_step, mesh=mesh, in_specs=(row_spec, P(), P(), P(), P(), row_spec, row_spec), out_specs=(row_spec, buf_spec), check_vma=False)
```

time: 48.6 us -> 42.9 us (0.88)
  Pallas kernels: 45.2 us -> 42.1 us
  local copies, waits for them, and re-layouts: 2.29 us -> 0 us
    pallas_call x1, Pallas kernels: 41.8 us -> 38.8 us  [device_step(): pl.pallas_call(functools.partial(block_kernel, side), out_shape=(pltpu.VM...]
    unnamed x5 -> x0, local copies, waits for them, and re-layouts: 2.29 us -> none
where the time goes in v2:
time: 42.9 us; the launch traced here: 42.8 us
  Pallas kernels  42.1 us (98%)
  between operations  0.64 us (1%)
    pallas_call x1, Pallas kernels, device_step(): pl.pallas_call(functools.partial(block_kernel, side), out_shape=(pltpu.VM...  38.8 us
    pallas_call x1, Pallas kernels, device_step(): pl.pallas_call(store_kernel, out_shape=(jax.ShapeDtypeStruct((own, tok *...  3.38 us

profile of v2, /device:TPU:97, one launch (start us, length us, event | category | flops | bytes accessed | tf_op | source)
XLA Modules:
  0.0 42.8 jit_solution(16700315959844910466)
XLA Ops:
  0.6 38.8 %attention_block.1 = (bf16[4,512,2048]{2,1,0:T(8,128)(2,1)S(1)}, bf16[16,2048]{1,0:T(8,128)(2,1)S(1)}) custom-call(bf16[16,2048]{1,0:T(8,128)(2,1)} %x_hbm.1, bf16[2048,4096]{1,0:T(8,128)(2,1)} %wq_hbm.1, bf16[2048,512]{1,0:T(8,128)(2,1)} %wk_hbm.1, bf16[2048,512]{1,0:T(8,128)(2,1)} %wv_hbm.1, bf16[4096,2048]{1,0:T(8,128)(2,1)} %wo_hbm.1, s32[2,16]{1,0:T(2,128)} %bitcast.1, ...), custom_call_target="tpu_custom_call" | custom-call | tf_op jit(solution)/shard_map/attention_block/pallas_call | solution.py:374
  39.4 3.4 %store_outputs.1 = (bf16[4,512,2048]{2,1,0:T(8,128)(2,1)}, bf16[16,2048]{1,0:T(8,128)(2,1)}) custom-call(bf16[4,512,2048]{2,1,0:T(8,128)(2,1)S(1)} %get-tuple-element.6.buf_ref, bf16[16,2048]{1,0:T(8,128)(2,1)S(1)} %get-tuple-element.7.h_ref), custom_call_target="tpu_custom_call" | custom-call | tf_op jit(solution)/shard_map/store_outputs/pallas_call | solution.py:407

commit v3 on v2

--- a/solution.py
+++ b/solution.py
@@ -22,7 +22,7 @@
                  buf_out, h_out,
                  xbuf, wq_v, wk_v, wv_v, wo_v, ids_v, probs_v, kv_own, kvbuf, meta_own, meta_buf, q_s, o_own, o_sib,
                  h_buf, sel_s, gate_s,
-                 wsem, pair_send, pair_recv, kv_send, kv_recv, mt_send, mt_recv, h_send, h_recv,
+                 wsem, pair_send, pair_recv, kv_send, kv_recv, kv2_send, kv2_recv, mt_send, mt_recv, h_send, h_recv,
                  d_send, d_recv):
     tok = x_hbm.shape[0]
     tok2 = CORES * tok
@@ -35,7 +35,6 @@
     own_experts = buf_out.shape[0]
     experts = probs_v.shape[1]
     n_chips = side * side
-    n_dev = n_chips * CORES
 
     me = lax.axis_index('sp')
     core = me % CORES
@@ -83,8 +82,13 @@
     kvbuf[...] = jnp.zeros_like(kvbuf)
 
     barrier = pltpu.get_barrier_semaphore()
-    for i in range(1, n_dev):
-        pl.semaphore_signal(barrier, inc=1, device_id={'sp': (me + i) % n_dev}, device_id_type=MESH_IDS)
+    partners = [sib]
+    for d in range(1, side):
+        for c in range(CORES):
+            partners.append({'sp': (cy * side + (cx + d) % side) * CORES + c})
+            partners.append({'sp': ((cy + d) % side * side + cx) * CORES + c})
+    for p in partners:
+        pl.semaphore_signal(barrier, inc=1, device_id=p, device_id_type=MESH_IDS)
 
     loads['x'].wait()
     loads['ids'].wait()
@@ -116,7 +120,7 @@
             kv_own[c, :, at:at + half_kv] = out[:, c * half_kv:(c + 1) * half_kv]
     kvbuf[chip, my_rows, :] = kv_own[core]
 
-    pl.semaphore_wait(barrier, n_dev - 1)
+    pl.semaphore_wait(barrier, len(partners))
     x_pair = remote(xbuf.at[my_rows, :], xbuf.at[my_rows, :], pair_send.at[0], pair_recv.at[0], sib)
     x_pair.start()
     m_pair = remote(meta_own.at[0], meta_own.at[1], pair_send.at[1], pair_recv.at[1], sib)
@@ -124,15 +128,20 @@
     kv_pair = remote(kv_own.at[1 - core], kvbuf.at[chip, my_rows, :], pair_send.at[2], pair_recv.at[2], sib)
     kv_pair.start()
 
-    def kv_copy(k, c, slot, rows, src_core):
-        return remote(kv_own.at[c], kvbuf.at[slot, rows, :], kv_send.at[CORES * k + c],
-                      kv_recv.at[CORES * k + src_core], {'sp': (chip + k) % n_chips * CORES + c})
-
-    for k in range(1, n_chips):
-        @pl.when(chip + k < n_chips)
-        def _():
-            for c in range(CORES):
-                kv_copy(k, c, chip, my_rows, core).start()
+    def kv_first(d, c):
+        y = (cy + d * c) % side
+        x = (cx + d * (1 - c)) % side
+        i = cx + (cy - cx) * c
+        return remote(kv_own.at[c], kvbuf.at[chip, my_rows, :], kv_send.at[CORES * d + c],
+                      kv_recv.at[CORES * i + core], {'sp': (y * side + x) * CORES + c})
+
+    def kv_first_from(i, c):
+        return remote(kv_own.at[c], kvbuf.at[chip_at(i, b0), pl.ds(c * tok, tok), :], kv_send.at[0],
+                      kv_recv.at[CORES * i + c], sib)
+
+    for d in (2, 1, side - 1):
+        for c in range(CORES):
+            kv_first(d, c).start()
 
     class Gather:
         def __init__(self, ref, ss, rs):
@@ -153,12 +162,12 @@
             return remote(self.ref(slot), self.ref(slot), self.ss.at[0], self.rs.at[side + i * side + j], sib)
 
         def open(self):
-            for d in (1, side - 1, 2):
+            for d in (2, 1, side - 1):
                 self.first(d, chip).start()
             self.spread(a0)
 
         def spread(self, i):
-            for d in (1, side - 1, 2):
+            for d in (2, 1, side - 1):
                 self.second(i, d, chip_at(i, b0)).start()
 
         def sent(self):
@@ -166,6 +175,22 @@
                 self.first(d, chip).wait_send()
                 for i in range(side):
                     self.second(i, d, chip_at(i, b0)).wait_send()
+
+    kvg = Gather(lambda s: kvbuf.at[s], kv2_send, kv2_recv)
+
+    def kv_second(i, wait):
+        slot = chip_at(i, b0)
+        for d in (2, 1, side - 1):
+            @pl.when(chip_at(a0, (b0 + d) % side) > slot)
+            def _():
+                c = kvg.second(i, d, slot)
+                if wait:
+                    c.wait_send()
+                else:
+                    c.start()
+
+    kv_pair.wait_recv()
+    kv_second(a0, False)
 
     x_pair.wait_recv()
     xs = xbuf[...]
@@ -179,12 +204,25 @@
     mt = Gather(lambda s: meta_buf.at[s], mt_send, mt_recv)
     mt.open()
 
-    kv_pair.wait_recv()
-    for k in range(1, n_chips):
-        @pl.when(chip >= k)
+    def kv_pass(i, carry):
+        @pl.when(i != a0)
         def _():
             for c in range(CORES):
-                kv_copy(k, c, chip - k, pl.ds(c * tok, tok), c).wait_recv()
+                kv_first_from(i, c).wait_recv()
+            kv_second(i, False)
+        return carry
+
+    lax.fori_loop(0, side, kv_pass, 0)
+
+    def kv_done(n, carry):
+        i, j = n // side, n % side
+
+        @pl.when((j != b0) & (chip_at(i, j) < chip))
+        def _():
+            kvg.second_from(i, j, chip_at(i, j)).wait_recv()
+        return carry
+
+    lax.fori_loop(0, n_chips, kv_done, 0)
 
     seq = n_chips * tok2
     q_pos = chip * tok2 + lax.broadcasted_iota(jnp.int32, (per_kv * tok2, seq), 0) % tok2
@@ -329,11 +367,11 @@
 
     for c in [x_pair, m_pair, kv_pair] + o_pairs:
         c.wait_send()
-    for k in range(1, n_chips):
-        @pl.when(chip + k < n_chips)
-        def _():
-            for c in range(CORES):
-                kv_copy(k, c, chip, my_rows, core).wait_send()
+    for d in range(1, side):
+        for c in range(CORES):
+            kv_first(d, c).wait_send()
+    for i in range(side):
+        kv_second(i, True)
     mt.sent()
     hg.sent()
     for slot in range(n_chips):
@@ -396,8 +434,9 @@
                 pltpu.VMEM((chips, own * tok2, LANES), F32),
                 dma((n_loads,)),
                 dma((3 + kv_half_heads,)), dma((3 + kv_half_heads,)),
-                dma((group,)), dma((group,)),
+                dma((CORES * side,)), dma((CORES * side,)),
                 dma((side + chips,)), dma((side + chips,)), dma((side + chips,)), dma((side + chips,)),
+                dma((side + chips,)), dma((side + chips,)),
                 dma((chips,)), dma((chips,)),
             ],
             compiler_params=pltpu.CompilerParams(collective_id=0, has_side_effects=True,

time: 42.9 us -> 41.3 us (0.963)
  Pallas kernels: 42.1 us -> 40.5 us
    pallas_call x1, Pallas kernels: 38.8 us -> 37.2 us  [device_step(): pl.pallas_call(functools.partial(block_kernel, side), out_shape=(pltpu.VM...]
where the time goes in v3:
time: 41.3 us; the launch traced here: 41.2 us
  Pallas kernels  40.5 us (98%)
  between operations  0.64 us (2%)
    pallas_call x1, Pallas kernels, device_step(): pl.pallas_call(functools.partial(block_kernel, side), out_shape=(pltpu.VM...  37.2 us
    pallas_call x1, Pallas kernels, device_step(): pl.pallas_call(store_kernel, out_shape=(jax.ShapeDtypeStruct((own, tok *...  3.38 us

profile of v3, /device:TPU:97, one launch (start us, length us, event | category | flops | bytes accessed | tf_op | source)
XLA Modules:
  0.0 41.2 jit_solution(1891298976539304465)
XLA Ops:
  0.6 37.2 %attention_block.1 = (bf16[4,512,2048]{2,1,0:T(8,128)(2,1)S(1)}, bf16[16,2048]{1,0:T(8,128)(2,1)S(1)}) custom-call(bf16[16,2048]{1,0:T(8,128)(2,1)} %x_hbm.1, bf16[2048,4096]{1,0:T(8,128)(2,1)} %wq_hbm.1, bf16[2048,512]{1,0:T(8,128)(2,1)} %wk_hbm.1, bf16[2048,512]{1,0:T(8,128)(2,1)} %wv_hbm.1, bf16[4096,2048]{1,0:T(8,128)(2,1)} %wo_hbm.1, s32[2,16]{1,0:T(2,128)} %bitcast.1, ...), custom_call_target="tpu_custom_call" | custom-call | tf_op jit(solution)/shard_map/attention_block/pallas_call | solution.py:412
  37.8 3.4 %store_outputs.1 = (bf16[4,512,2048]{2,1,0:T(8,128)(2,1)}, bf16[16,2048]{1,0:T(8,128)(2,1)}) custom-call(bf16[4,512,2048]{2,1,0:T(8,128)(2,1)S(1)} %get-tuple-element.6.buf_ref, bf16[16,2048]{1,0:T(8,128)(2,1)S(1)} %get-tuple-element.7.h_ref), custom_call_target="tpu_custom_call" | custom-call | tf_op jit(solution)/shard_map/store_outputs/pallas_call | solution.py:446

commit v4 on v3

--- a/solution.py
+++ b/solution.py
@@ -14,6 +14,7 @@
 LANES = 128
 CORES = 2
 Q_COLS = 512
+B_COLS = 256
 F32 = jnp.float32
 BF16 = jnp.bfloat16
 
@@ -58,6 +59,15 @@
         return pltpu.make_async_remote_copy(src_ref=src, dst_ref=dst, send_sem=ss, recv_sem=rs,
                                             device_id=dev, device_id_type=MESH_IDS)
 
+    barrier = pltpu.get_barrier_semaphore()
+    partners = [sib]
+    for d in range(1, side):
+        for c in range(CORES):
+            partners.append({'sp': (cy * side + (cx + d) % side) * CORES + c})
+            partners.append({'sp': ((cy + d) % side * side + cx) * CORES + c})
+    for p in partners:
+        pl.semaphore_signal(barrier, inc=1, device_id=p, device_id_type=MESH_IDS)
+
     my_rows = pl.ds(pl.multiple_of(core * tok, tok), tok)
     loads = {}
 
@@ -79,16 +89,12 @@
     load('o1', wo_hbm.at[pl.ds(pl.multiple_of((1 - core) * half_q, half_q), half_q), o_cols],
          wo_v.at[pl.ds(half_q, half_q), :])
 
-    kvbuf[...] = jnp.zeros_like(kvbuf)
-
-    barrier = pltpu.get_barrier_semaphore()
-    partners = [sib]
-    for d in range(1, side):
-        for c in range(CORES):
-            partners.append({'sp': (cy * side + (cx + d) % side) * CORES + c})
-            partners.append({'sp': ((cy + d) % side * side + cx) * CORES + c})
-    for p in partners:
-        pl.semaphore_signal(barrier, inc=1, device_id=p, device_id_type=MESH_IDS)
+    for slot in range(n_chips):
+        y, x = slot // side, slot % side
+
+        @pl.when((slot > chip) & (y + (x - y) * core != b0))
+        def _():
+            kvbuf[slot] = jnp.zeros(kvbuf.shape[1:], BF16)
 
     loads['x'].wait()
     loads['ids'].wait()
@@ -104,7 +110,8 @@
     psum = p0 + p1
     lane_t = lax.broadcasted_iota(jnp.int32, (tok, LANES), 1)
     row_t = lax.broadcasted_iota(jnp.int32, (tok, LANES), 0)
-    eye = lane_t == row_t + core * tok
+    per_group = LANES // tok2
+    eye = lane_t == row_t + core * tok + chip % per_group * tok2
 
     def to_lanes(col):
         return jnp.sum(jnp.where(eye, col, 0.0), axis=0, keepdims=True)
@@ -157,6 +164,12 @@
         def second(self, i, d, slot):
             return remote(self.ref(slot), self.ref(slot), self.ss.at[side + i * side + d],
                           self.rs.at[side + i * side + b0], peer(chip_at(a0, (b0 + d) % side)))
+
+        def relay(self, i, step):
+            j = (b0 - step + side) % side
+            slot = chip_at(i, j)
+            return remote(self.ref(slot), self.ref(slot), self.ss.at[side + i * side + 2],
+                          self.rs.at[side + i * side + j], peer(chip_at(a0, (b0 + step + side) % side)))
 
         def second_from(self, i, j, slot):
             return remote(self.ref(slot), self.ref(slot), self.ss.at[0], self.rs.at[side + i * side + j], sib)
@@ -191,6 +204,10 @@
 
     kv_pair.wait_recv()
     kv_second(a0, False)
+    m_pair.wait_recv()
+    meta_buf[chip] = meta_own[0] + meta_own[1]
+    mt = Gather(lambda s: meta_buf.at[s], mt_send, mt_recv)
+    mt.open()
 
     x_pair.wait_recv()
     xs = xbuf[...]
@@ -199,17 +216,14 @@
         cols = slice(i * Q_COLS, (i + 1) * Q_COLS)
         q_s[:, cols] = jnp.dot(xs, wq_v[:, cols], preferred_element_type=F32).astype(BF16)
 
-    m_pair.wait_recv()
-    meta_buf[chip] = meta_own[0] + meta_own[1]
-    mt = Gather(lambda s: meta_buf.at[s], mt_send, mt_recv)
-    mt.open()
-
     def kv_pass(i, carry):
         @pl.when(i != a0)
         def _():
             for c in range(CORES):
                 kv_first_from(i, c).wait_recv()
             kv_second(i, False)
+            mt.first_from(i, chip_at(i, b0)).wait_recv()
+            mt.spread(i)
         return carry
 
     lax.fori_loop(0, side, kv_pass, 0)
@@ -249,15 +263,6 @@
         c.start()
         o_pairs.append(c)
 
-    def pass_meta(i, carry):
-        @pl.when(i != a0)
-        def _():
-            mt.first_from(i, chip_at(i, b0)).wait_recv()
-            mt.spread(i)
-        return carry
-
-    lax.fori_loop(0, side, pass_meta, 0)
-
     loads['o0'].wait()
     acc = jnp.dot(o_own[...], wo_v[0:half_q, :], preferred_element_type=F32)
     loads['o1'].wait()
@@ -270,12 +275,26 @@
     hg = Gather(lambda s: h_buf.at[core, s], h_send, h_recv)
 
     def cross(slot):
-        return remote(h_buf.at[core, slot], h_buf.at[core, slot], d_send.at[slot], d_recv.at[slot], sib)
+        at = h_buf.at[core, slot]
+        return remote(at, at, d_send.at[slot], d_recv.at[slot], sib)
 
     def cross_from(slot):
-        return remote(h_buf.at[1 - core, slot], h_buf.at[1 - core, slot], d_send.at[slot], d_recv.at[slot], sib)
-
-    hg.open()
+        at = h_buf.at[1 - core, slot]
+        return remote(at, at, d_send.at[slot], d_recv.at[slot], sib)
+
+    relays = ((0, 1), (1, -1), (3, -1))
+
+    def h_spread(k):
+        i = (a0 - k + side) % side
+        slot = chip_at(i, b0)
+        for d in (1, side - 1):
+            hg.second(i, d, slot).start()
+        if k == 2:
+            hg.second(i, 2, slot).start()
+
+    for d in (1, side - 1, 2):
+        hg.first(d, chip).start()
+    h_spread(0)
     cross(chip).start()
 
     def meta_done(n, carry):
@@ -288,82 +307,98 @@
 
     lax.fori_loop(0, n_chips, meta_done, 0)
 
-    lane_1 = lax.broadcasted_iota(jnp.int32, (1, LANES), 1)
-    t_row = lax.broadcasted_iota(jnp.int32, (LANES, LANES), 0)
-    t_col = lax.broadcasted_iota(jnp.int32, (LANES, LANES), 1)
+    g_tok = per_group * tok2
+    n_groups = n_chips // per_group
+    t_row = lax.broadcasted_iota(jnp.int32, (g_tok, g_tok), 0)
+    t_col = lax.broadcasted_iota(jnp.int32, (g_tok, g_tok), 1)
     before = jnp.where((t_row < t_col) & (t_row // tok == t_col // tok), 1.0, 0.0).astype(BF16)
-    source_base = ((lane_1 // tok) * tok).astype(F32)
-    live = lane_1 < tok2
-    slot_row = lax.broadcasted_iota(jnp.int32, (tok2, LANES), 0).astype(F32)
-
-    def select_rows(s, carry):
-        m = meta_buf[s]
-        e_first, e_second = m[0:1, :], m[1:2, :]
-        sels, gates = [], []
+    lane_8 = lax.broadcasted_iota(jnp.int32, (8, g_tok), 1)
+    source_base = (lane_8 // tok * tok).astype(F32)
+    expert_8 = (lax.broadcasted_iota(jnp.int32, (8, g_tok), 0) + me * own_experts).astype(F32)
+    slot_row = t_row.astype(F32)
+
+    def select_rows(g, carry):
+        m = meta_buf[g * per_group]
+        for c in range(1, per_group):
+            m = m + meta_buf[g * per_group + c]
+        hit0 = m[0:1, :] == expert_8
+        hit1 = m[1:2, :] == expert_8
+        hit = hit0 | hit1
+        slot = jnp.dot(jnp.where(hit, 1.0, 0.0).astype(BF16), before, preferred_element_type=F32)
+        row = jnp.where(hit, slot + source_base, -1.0)
+        gate = jnp.where(hit0, m[2:3, :], jnp.where(hit1, m[3:4, :], 0.0))
         for k in range(own_experts):
-            expert = (me * own_experts + k).astype(F32)
-            hit0 = (e_first == expert) & live
-            hit1 = (e_second == expert) & live
-            hit = jnp.where(hit0 | hit1, 1.0, 0.0)
-            slot = jnp.dot(jnp.broadcast_to(hit, (8, LANES)).astype(BF16), before, preferred_element_type=F32)[0:1, :]
-            row = jnp.where(hit0 | hit1, slot + source_base, -1.0)
-            gate = jnp.where(hit0, m[2:3, :], jnp.where(hit1, m[3:4, :], 0.0))
-            pick = slot_row == row
-            sels.append(jnp.where(pick, 1.0, 0.0))
-            gates.append(jnp.broadcast_to(jnp.sum(jnp.where(pick, gate, 0.0), axis=1, keepdims=True), (tok2, LANES)))
-        sel_s[s] = jnp.concatenate(sels, axis=0).astype(BF16)
-        gate_s[s] = jnp.concatenate(gates, axis=0)
+            rows = pl.ds(k * g_tok, g_tok)
+            pick = slot_row == row[k:k + 1, :]
+            sel_s[g, rows, :] = jnp.where(pick, 1.0, 0.0).astype(BF16)
+            gate_k = jnp.sum(jnp.where(pick, gate[k:k + 1, :], 0.0), axis=1, keepdims=True)
+            gate_s[g, rows, :] = jnp.broadcast_to(gate_k, (g_tok, LANES))
         return carry
 
-    lax.fori_loop(0, n_chips, select_rows, 0)
-
-    def build(slot, col_half):
-        sel = sel_s[slot][:, 0:tok2]
-        rows = jnp.dot(sel, h_buf[col_half, slot], preferred_element_type=F32)
-        gate = gate_s[slot]
-        rows = jnp.concatenate([rows[:, i * LANES:(i + 1) * LANES] * gate for i in range(half_w // LANES)], axis=1)
-        rows = rows.astype(BF16)
-        at = pl.ds(pl.multiple_of(slot * tok2, tok2), tok2)
-        cols = pl.ds(pl.multiple_of(col_half * half_w, half_w), half_w)
-        for k in range(own_experts):
-            buf_out[k, at, cols] = rows[k * tok2:(k + 1) * tok2, :]
-
-    build(chip, core)
-
-    def pass_first(i, carry):
-        @pl.when(i != a0)
-        def _():
-            slot = chip_at(i, b0)
-            hg.first_from(i, slot).wait_recv()
-            hg.spread(i)
-            cross(slot).start()
-            build(slot, core)
+    lax.fori_loop(0, n_groups, select_rows, 0)
+
+    def build(g, col_half):
+        at = pl.ds(pl.multiple_of(g * g_tok, g_tok), g_tok)
+        h_g = h_buf[col_half, pl.ds(g * per_group, per_group)].reshape(g_tok, half_w)
+        for n in range(half_w // B_COLS):
+            rows = jnp.dot(sel_s[g], h_g[:, n * B_COLS:(n + 1) * B_COLS], preferred_element_type=F32)
+            gate = gate_s[g]
+            rows = jnp.concatenate([rows[:, i * LANES:(i + 1) * LANES] * gate for i in range(B_COLS // LANES)], axis=1)
+            rows = rows.astype(BF16)
+            cols = pl.ds(pl.multiple_of(col_half * half_w + n * B_COLS, B_COLS), B_COLS)
+            for k in range(own_experts):
+                buf_out[k, at, cols] = rows[k * g_tok:(k + 1) * g_tok, :]
+
+    def take_first(k):
+        i = (a0 - k + side) % side
+        slot = chip_at(i, b0)
+        hg.first_from(i, slot).wait_recv()
+        h_spread(k)
+        cross(slot).start()
+
+    def take_relay(k, step):
+        i = (a0 - k + side) % side
+        j = (b0 - step + side) % side
+        slot = chip_at(i, j)
+        hg.second_from(i, j, slot).wait_recv()
+        hg.relay(i, step).start()
+        cross(slot).start()
+
+    take_first(1)
+    take_first(side - 1)
+    take_relay(*relays[0])
+    take_first(2)
+    take_relay(*relays[1])
+    take_relay(*relays[2])
+
+    def take_rest(g, carry):
+        @pl.when(g < n_groups)
+        def _():
+            for c in range(per_group):
+                slot = g * per_group + c
+                y, x = slot // side, slot % side
+                i = x + (y - x) * core
+                j = y + (x - y) * core
+                todo = j != b0
+                for k, step in relays:
+                    todo = todo & ((i != (a0 - k + side) % side) | (j != (b0 - step + side) % side))
+
+                @pl.when(todo)
+                def _():
+                    hg.second_from(i, j, slot).wait_recv()
+                    cross(slot).start()
+            build(g, core)
+
+        @pl.when(g > 0)
+        def _():
+            for c in range(per_group):
+                cross_from((g - 1) * per_group + c).wait_recv()
+            build(g - 1, 1 - core)
         return carry
 
-    lax.fori_loop(0, side, pass_first, 0)
-
-    lag = side
-
-    def pass_second(slot, carry):
-        y, x = slot // side, slot % side
-        i = x + (y - x) * core
-        j = y + (x - y) * core
-
-        @pl.when((slot < n_chips) & (j != b0))
-        def _():
-            hg.second_from(i, j, slot).wait_recv()
-            cross(slot).start()
-            build(slot, core)
-
-        @pl.when(slot >= lag)
-        def _():
-            cross_from(slot - lag).wait_recv()
-            build(slot - lag, 1 - core)
-        return carry
-
-    lax.fori_loop(0, n_chips + lag, pass_second, 0)
-    h_out[:, 0:half_w] = h_buf[0, chip, my_rows, :]
-    h_out[:, half_w:2 * half_w] = h_buf[1, chip, my_rows, :]
+    lax.fori_loop(0, n_groups + 1, take_rest, 0)
+    for c in range(CORES):
+        h_out[:, c * half_w:(c + 1) * half_w] = h_buf[c, chip, my_rows, :]
 
     for c in [x_pair, m_pair, kv_pair] + o_pairs:
         c.wait_send()
@@ -430,8 +465,8 @@
                 pltpu.VMEM((tok2, half_q), BF16),
                 pltpu.VMEM((tok2, half_q), BF16),
                 pltpu.VMEM((CORES, chips, tok2, half_w), BF16),
-                pltpu.VMEM((chips, own * tok2, LANES), BF16),
-                pltpu.VMEM((chips, own * tok2, LANES), F32),
+                pltpu.VMEM((chips * tok2 // LANES, own * LANES, LANES), BF16),
+                pltpu.VMEM((chips * tok2 // LANES, own * LANES, LANES), F32),
                 dma((n_loads,)),
                 dma((3 + kv_half_heads,)), dma((3 + kv_half_heads,)),
                 dma((CORES * side,)), dma((CORES * side,)),

time: 41.3 us -> 39.7 us (0.961)
  Pallas kernels: 40.5 us -> 38.9 us
    pallas_call x1, Pallas kernels: 37.2 us -> 35.6 us  [device_step(): pl.pallas_call(functools.partial(block_kernel, side), out_shape=(pltpu.VM...]
where the time goes in v4:
time: 39.7 us; the launch traced here: 39.6 us
  Pallas kernels  38.9 us (98%)
  between operations  0.64 us (2%)
    pallas_call x1, Pallas kernels, device_step(): pl.pallas_call(functools.partial(block_kernel, side), out_shape=(pltpu.VM...  35.6 us
    pallas_call x1, Pallas kernels, device_step(): pl.pallas_call(store_kernel, out_shape=(jax.ShapeDtypeStruct((own, tok *...  3.38 us

profile of v4, /device:TPU:97, one launch (start us, length us, event | category | flops | bytes accessed | tf_op | source)
XLA Modules:
  0.0 39.6 jit_solution(1689586358817164505)
XLA Ops:
  0.6 35.6 %attention_block.1 = (bf16[4,512,2048]{2,1,0:T(8,128)(2,1)S(1)}, bf16[16,2048]{1,0:T(8,128)(2,1)S(1)}) custom-call(bf16[16,2048]{1,0:T(8,128)(2,1)} %x_hbm.1, bf16[2048,4096]{1,0:T(8,128)(2,1)} %wq_hbm.1, bf16[2048,512]{1,0:T(8,128)(2,1)} %wk_hbm.1, bf16[2048,512]{1,0:T(8,128)(2,1)} %wv_hbm.1, bf16[4096,2048]{1,0:T(8,128)(2,1)} %wo_hbm.1, s32[2,16]{1,0:T(2,128)} %bitcast.1, ...), custom_call_target="tpu_custom_call" | custom-call | tf_op jit(solution)/shard_map/attention_block/pallas_call | solution.py:447
  36.2 3.4 %store_outputs.1 = (bf16[4,512,2048]{2,1,0:T(8,128)(2,1)}, bf16[16,2048]{1,0:T(8,128)(2,1)}) custom-call(bf16[4,512,2048]{2,1,0:T(8,128)(2,1)S(1)} %get-tuple-element.6.buf_ref, bf16[16,2048]{1,0:T(8,128)(2,1)S(1)} %get-tuple-element.7.h_ref), custom_call_target="tpu_custom_call" | custom-call | tf_op jit(solution)/shard_map/store_outputs/pallas_call | solution.py:481

commit v5 on v4

--- a/solution.py
+++ b/solution.py
@@ -14,6 +14,7 @@
 LANES = 128
 CORES = 2
 Q_COLS = 512
+Q_EARLY = 0
 B_COLS = 256
 F32 = jnp.float32
 BF16 = jnp.bfloat16
@@ -110,14 +111,12 @@
     psum = p0 + p1
     lane_t = lax.broadcasted_iota(jnp.int32, (tok, LANES), 1)
     row_t = lax.broadcasted_iota(jnp.int32, (tok, LANES), 0)
-    per_group = LANES // tok2
-    eye = lane_t == row_t + core * tok + chip % per_group * tok2
-
-    def to_lanes(col):
-        return jnp.sum(jnp.where(eye, col, 0.0), axis=0, keepdims=True)
-
-    meta_rows = [to_lanes(id0), to_lanes(id1), to_lanes(p0 / psum), to_lanes(p1 / psum)]
-    meta_own[0] = jnp.concatenate(meta_rows + [jnp.zeros((4, LANES), F32)], axis=0)
+    meta_rows = []
+    for place in (cx, cy):
+        eye = lane_t == row_t + core * tok + place * tok2
+        for col in (id0, id1, p0 / psum, p1 / psum):
+            meta_rows.append(jnp.sum(jnp.where(eye, col, 0.0), axis=0, keepdims=True))
+    meta_own[0] = jnp.concatenate(meta_rows, axis=0)
 
     x_own = xbuf[my_rows, :]
     for name, w_ref, at in (('k', wk_v, 0), ('v', wv_v, half_kv)):
@@ -154,49 +153,49 @@
         def __init__(self, ref, ss, rs):
             self.ref, self.ss, self.rs = ref, ss, rs
 
-        def first(self, d, slot):
-            return remote(self.ref(slot), self.ref(slot), self.ss.at[d], self.rs.at[a0],
-                          peer(chip_at((a0 + d) % side, b0)))
-
-        def first_from(self, i, slot):
-            return remote(self.ref(slot), self.ref(slot), self.ss.at[0], self.rs.at[i], sib)
-
-        def second(self, i, d, slot):
-            return remote(self.ref(slot), self.ref(slot), self.ss.at[side + i * side + d],
-                          self.rs.at[side + i * side + b0], peer(chip_at(a0, (b0 + d) % side)))
+        def copy(self, i, j, s, r, dev):
+            return remote(self.ref(i, j), self.ref(i, j), self.ss.at[s], self.rs.at[r], dev)
+
+        def first(self, d):
+            return self.copy(a0, b0, d, a0, peer(chip_at((a0 + d) % side, b0)))
+
+        def first_from(self, i):
+            return self.copy(i, b0, 0, i, sib)
+
+        def second(self, i, d):
+            return self.copy(i, b0, side + i * side + d, side + i * side + b0, peer(chip_at(a0, (b0 + d) % side)))
 
         def relay(self, i, step):
             j = (b0 - step + side) % side
-            slot = chip_at(i, j)
-            return remote(self.ref(slot), self.ref(slot), self.ss.at[side + i * side + 2],
-                          self.rs.at[side + i * side + j], peer(chip_at(a0, (b0 + step + side) % side)))
-
-        def second_from(self, i, j, slot):
-            return remote(self.ref(slot), self.ref(slot), self.ss.at[0], self.rs.at[side + i * side + j], sib)
+            return self.copy(i, j, side + i * side + 2, side + i * side + j,
+                             peer(chip_at(a0, (b0 + step + side) % side)))
+
+        def second_from(self, i, j):
+            return self.copy(i, j, 0, side + i * side + j, sib)
 
         def open(self):
             for d in (2, 1, side - 1):
-                self.first(d, chip).start()
+                self.first(d).start()
             self.spread(a0)
 
         def spread(self, i):
             for d in (2, 1, side - 1):
-                self.second(i, d, chip_at(i, b0)).start()
+                self.second(i, d).start()
 
         def sent(self):
             for d in range(1, side):
-                self.first(d, chip).wait_send()
+                self.first(d).wait_send()
                 for i in range(side):
-                    self.second(i, d, chip_at(i, b0)).wait_send()
-
-    kvg = Gather(lambda s: kvbuf.at[s], kv2_send, kv2_recv)
+                    self.second(i, d).wait_send()
+
+    kvg = Gather(lambda i, j: kvbuf.at[chip_at(i, j)], kv2_send, kv2_recv)
 
     def kv_second(i, wait):
         slot = chip_at(i, b0)
         for d in (2, 1, side - 1):
             @pl.when(chip_at(a0, (b0 + d) % side) > slot)
             def _():
-                c = kvg.second(i, d, slot)
+                c = kvg.second(i, d)
                 if wait:
                     c.wait_send()
                 else:
@@ -206,15 +205,17 @@
     kv_second(a0, False)
     m_pair.wait_recv()
     meta_buf[chip] = meta_own[0] + meta_own[1]
-    mt = Gather(lambda s: meta_buf.at[s], mt_send, mt_recv)
+    mt = Gather(lambda i, j: meta_buf.at[chip_at(i, j)], mt_send, mt_recv)
     mt.open()
 
+    def project_q(chunks):
+        for n in chunks:
+            loads[('q', n)].wait()
+            cols = slice(n * Q_COLS, (n + 1) * Q_COLS)
+            q_s[:, cols] = jnp.dot(xbuf[...], wq_v[:, cols], preferred_element_type=F32).astype(BF16)
+
     x_pair.wait_recv()
-    xs = xbuf[...]
-    for i in range(n_q):
-        loads[('q', i)].wait()
-        cols = slice(i * Q_COLS, (i + 1) * Q_COLS)
-        q_s[:, cols] = jnp.dot(xs, wq_v[:, cols], preferred_element_type=F32).astype(BF16)
+    project_q(range(Q_EARLY))
 
     def kv_pass(i, carry):
         @pl.when(i != a0)
@@ -222,18 +223,20 @@
             for c in range(CORES):
                 kv_first_from(i, c).wait_recv()
             kv_second(i, False)
-            mt.first_from(i, chip_at(i, b0)).wait_recv()
+            mt.first_from(i).wait_recv()
             mt.spread(i)
         return carry
 
     lax.fori_loop(0, side, kv_pass, 0)
 
+    project_q(range(Q_EARLY, n_q))
+
     def kv_done(n, carry):
         i, j = n // side, n % side
 
         @pl.when((j != b0) & (chip_at(i, j) < chip))
         def _():
-            kvg.second_from(i, j, chip_at(i, j)).wait_recv()
+            kvg.second_from(i, j).wait_recv()
         return carry
 
     lax.fori_loop(0, n_chips, kv_done, 0)
@@ -270,45 +273,43 @@
         c.wait_recv()
     acc = acc + jnp.dot(o_sib[...], wo_v[half_q:2 * half_q, :], preferred_element_type=F32)
     my_cols = pl.ds(pl.multiple_of(core * half_w, half_w), half_w)
-    h_buf[core, chip] = (xbuf[:, my_cols].astype(F32) + acc).astype(BF16)
-
-    hg = Gather(lambda s: h_buf.at[core, s], h_send, h_recv)
-
-    def cross(slot):
-        at = h_buf.at[core, slot]
-        return remote(at, at, d_send.at[slot], d_recv.at[slot], sib)
-
-    def cross_from(slot):
-        at = h_buf.at[1 - core, slot]
-        return remote(at, at, d_send.at[slot], d_recv.at[slot], sib)
-
-    relays = ((0, 1), (1, -1), (3, -1))
+    h_buf[core, b0 * side + a0] = (xbuf[:, my_cols].astype(F32) + acc).astype(BF16)
+
+    hg = Gather(lambda i, j: h_buf.at[core, j * side + i], h_send, h_recv)
+
+    def cross(i, j):
+        at = h_buf.at[core, j * side + i]
+        return remote(at, at, d_send.at[j * side + i], d_recv.at[j * side + i], sib)
+
+    def cross_from(n):
+        at = h_buf.at[1 - core, n]
+        return remote(at, at, d_send.at[n], d_recv.at[n], sib)
+
+    relays = {0: 1, 1: -1, side - 1: -1}
+
+    def back(at, d):
+        return (at - d + side) % side
 
     def h_spread(k):
-        i = (a0 - k + side) % side
-        slot = chip_at(i, b0)
-        for d in (1, side - 1):
-            hg.second(i, d, slot).start()
-        if k == 2:
-            hg.second(i, 2, slot).start()
+        for d in (1, side - 1) if k in relays else (1, side - 1, 2):
+            hg.second(back(a0, k), d).start()
 
     for d in (1, side - 1, 2):
-        hg.first(d, chip).start()
+        hg.first(d).start()
     h_spread(0)
-    cross(chip).start()
+    cross(a0, b0).start()
 
     def meta_done(n, carry):
         i, j = n // side, n % side
 
         @pl.when(j != b0)
         def _():
-            mt.second_from(i, j, chip_at(i, j)).wait_recv()
+            mt.second_from(i, j).wait_recv()
         return carry
 
     lax.fori_loop(0, n_chips, meta_done, 0)
 
-    g_tok = per_group * tok2
-    n_groups = n_chips // per_group
+    g_tok = side * tok2
     t_row = lax.broadcasted_iota(jnp.int32, (g_tok, g_tok), 0)
     t_col = lax.broadcasted_iota(jnp.int32, (g_tok, g_tok), 1)
     before = jnp.where((t_row < t_col) & (t_row // tok == t_col // tok), 1.0, 0.0).astype(BF16)
@@ -318,87 +319,83 @@
     slot_row = t_row.astype(F32)
 
     def select_rows(g, carry):
-        m = meta_buf[g * per_group]
-        for c in range(1, per_group):
-            m = m + meta_buf[g * per_group + c]
-        hit0 = m[0:1, :] == expert_8
-        hit1 = m[1:2, :] == expert_8
-        hit = hit0 | hit1
-        slot = jnp.dot(jnp.where(hit, 1.0, 0.0).astype(BF16), before, preferred_element_type=F32)
-        row = jnp.where(hit, slot + source_base, -1.0)
-        gate = jnp.where(hit0, m[2:3, :], jnp.where(hit1, m[3:4, :], 0.0))
-        for k in range(own_experts):
-            rows = pl.ds(k * g_tok, g_tok)
-            pick = slot_row == row[k:k + 1, :]
-            sel_s[g, rows, :] = jnp.where(pick, 1.0, 0.0).astype(BF16)
-            gate_k = jnp.sum(jnp.where(pick, gate[k:k + 1, :], 0.0), axis=1, keepdims=True)
-            gate_s[g, rows, :] = jnp.broadcast_to(gate_k, (g_tok, LANES))
+        for half in range(CORES):
+            m = jnp.zeros((8, g_tok), F32)
+            for a in range(side):
+                m = m + meta_buf[a * side + g if half else g * side + a]
+            m = m[4 * half:4 * half + 4, :]
+            hit0 = m[0:1, :] == expert_8
+            hit1 = m[1:2, :] == expert_8
+            hit = hit0 | hit1
+            slot = jnp.dot(jnp.where(hit, 1.0, 0.0).astype(BF16), before, preferred_element_type=F32)
+            row = jnp.where(hit, slot + source_base, -1.0)
+            gate = jnp.where(hit0, m[2:3, :], jnp.where(hit1, m[3:4, :], 0.0))
+            for k in range(own_experts):
+                rows = pl.ds(k * g_tok, g_tok)
+                pick = slot_row == row[k:k + 1, :]
+                sel_s[half * side + g, rows, :] = jnp.where(pick, 1.0, 0.0).astype(BF16)
+                gate_k = jnp.sum(jnp.where(pick, gate[k:k + 1, :], 0.0), axis=1, keepdims=True)
+                gate_s[half * side + g, rows, :] = jnp.broadcast_to(gate_k, (g_tok, LANES))
         return carry
 
-    lax.fori_loop(0, n_groups, select_rows, 0)
-
-    def build(g, col_half):
-        at = pl.ds(pl.multiple_of(g * g_tok, g_tok), g_tok)
-        h_g = h_buf[col_half, pl.ds(g * per_group, per_group)].reshape(g_tok, half_w)
-        for n in range(half_w // B_COLS):
-            rows = jnp.dot(sel_s[g], h_g[:, n * B_COLS:(n + 1) * B_COLS], preferred_element_type=F32)
-            gate = gate_s[g]
+    lax.fori_loop(0, side, select_rows, 0)
+
+    def build(half, g):
+        n = half * side + g
+        for q in range(half_w // B_COLS):
+            h_g = h_buf[half, pl.ds(g * side, side), :, q * B_COLS:(q + 1) * B_COLS].reshape(g_tok, B_COLS)
+            rows = jnp.dot(sel_s[n], h_g, preferred_element_type=F32)
+            gate = gate_s[n]
             rows = jnp.concatenate([rows[:, i * LANES:(i + 1) * LANES] * gate for i in range(B_COLS // LANES)], axis=1)
             rows = rows.astype(BF16)
-            cols = pl.ds(pl.multiple_of(col_half * half_w + n * B_COLS, B_COLS), B_COLS)
-            for k in range(own_experts):
-                buf_out[k, at, cols] = rows[k * g_tok:(k + 1) * g_tok, :]
+            cols = pl.ds(pl.multiple_of(half * half_w + q * B_COLS, B_COLS), B_COLS)
+            for a in range(side):
+                slot = (g + (a - g) * half) * side + a + (g - a) * half
+                at = pl.ds(pl.multiple_of(slot * tok2, tok2), tok2)
+                for k in range(own_experts):
+                    buf_out[k, at, cols] = rows[k * g_tok + a * tok2:k * g_tok + (a + 1) * tok2, :]
 
     def take_first(k):
-        i = (a0 - k + side) % side
-        slot = chip_at(i, b0)
-        hg.first_from(i, slot).wait_recv()
+        i = back(a0, k)
+        hg.first_from(i).wait_recv()
         h_spread(k)
-        cross(slot).start()
-
-    def take_relay(k, step):
-        i = (a0 - k + side) % side
-        j = (b0 - step + side) % side
-        slot = chip_at(i, j)
-        hg.second_from(i, j, slot).wait_recv()
-        hg.relay(i, step).start()
-        cross(slot).start()
+        cross(i, b0).start()
+
+    def take(k, d):
+        i, j = back(a0, k), back(b0, d)
+        hg.second_from(i, j).wait_recv()
+        if k in relays and d == (relays[k] + side) % side:
+            hg.relay(i, relays[k]).start()
+        cross(i, j).start()
+
+    def build_other(d):
+        g = back(a0, d)
+        for a in range(side):
+            cross_from(g * side + a).wait_recv()
+        build(1 - core, g)
 
     take_first(1)
     take_first(side - 1)
-    take_relay(*relays[0])
+    take(0, 1)
     take_first(2)
-    take_relay(*relays[1])
-    take_relay(*relays[2])
-
-    def take_rest(g, carry):
-        @pl.when(g < n_groups)
-        def _():
-            for c in range(per_group):
-                slot = g * per_group + c
-                y, x = slot // side, slot % side
-                i = x + (y - x) * core
-                j = y + (x - y) * core
-                todo = j != b0
-                for k, step in relays:
-                    todo = todo & ((i != (a0 - k + side) % side) | (j != (b0 - step + side) % side))
-
-                @pl.when(todo)
-                def _():
-                    hg.second_from(i, j, slot).wait_recv()
-                    cross(slot).start()
-            build(g, core)
-
-        @pl.when(g > 0)
-        def _():
-            for c in range(per_group):
-                cross_from((g - 1) * per_group + c).wait_recv()
-            build(g - 1, 1 - core)
-        return carry
-
-    lax.fori_loop(0, n_groups + 1, take_rest, 0)
+    build(core, b0)
+    take(1, side - 1)
+    take(side - 1, side - 1)
+    for k in (1, side - 1, 2):
+        take(k, 1)
+    build(core, back(b0, 1))
+    build_other(0)
+    take(0, side - 1)
+    take(2, side - 1)
+    build(core, back(b0, side - 1))
+    build_other(1)
+    for k in (0, 2, 1, side - 1):
+        take(k, 2)
+    build_other(side - 1)
+    build(core, back(b0, 2))
+    build_other(2)
     for c in range(CORES):
-        h_out[:, c * half_w:(c + 1) * half_w] = h_buf[c, chip, my_rows, :]
+        h_out[:, c * half_w:(c + 1) * half_w] = h_buf[c, cx * side + cy if c else chip, my_rows, :]
 
     for c in [x_pair, m_pair, kv_pair] + o_pairs:
         c.wait_send()
@@ -409,8 +406,9 @@
         kv_second(i, True)
     mt.sent()
     hg.sent()
-    for slot in range(n_chips):
-        cross(slot).wait_send()
+    for i in range(side):
+        for j in range(side):
+            cross(i, j).wait_send()
 
 
 def store_kernel(buf_ref, h_ref, buf_out, h_out, sem):
@@ -465,8 +463,8 @@
                 pltpu.VMEM((tok2, half_q), BF16),
                 pltpu.VMEM((tok2, half_q), BF16),
                 pltpu.VMEM((CORES, chips, tok2, half_w), BF16),
-                pltpu.VMEM((chips * tok2 // LANES, own * LANES, LANES), BF16),
-                pltpu.VMEM((chips * tok2 // LANES, own * LANES, LANES), F32),
+                pltpu.VMEM((CORES * side, own * side * tok2, side * tok2), BF16),
+                pltpu.VMEM((CORES * side, own * side * tok2, LANES), F32),
                 dma((n_loads,)),
                 dma((3 + kv_half_heads,)), dma((3 + kv_half_heads,)),
                 dma((CORES * side,)), dma((CORES * side,)),

time: 39.7 us -> 39.3 us (0.990)
  no operation moved by 1% of the time
where the time goes in v5:
time: 39.3 us; the launch traced here: 39.2 us
  Pallas kernels  38.6 us (98%)
  between operations  0.64 us (2%)
    pallas_call x1, Pallas kernels, device_step(): pl.pallas_call(functools.partial(block_kernel, side), out_shape=(pltpu.VM...  35.2 us
    pallas_call x1, Pallas kernels, device_step(): pl.pallas_call(store_kernel, out_shape=(jax.ShapeDtypeStruct((own, tok *...  3.38 us

profile of v5, /device:TPU:97, one launch (start us, length us, event | category | flops | bytes accessed | tf_op | source)
XLA Modules:
  0.0 39.2 jit_solution(7357072739948728665)
XLA Ops:
  0.6 35.2 %attention_block.1 = (bf16[4,512,2048]{2,1,0:T(8,128)(2,1)S(1)}, bf16[16,2048]{1,0:T(8,128)(2,1)S(1)}) custom-call(bf16[16,2048]{1,0:T(8,128)(2,1)} %x_hbm.1, bf16[2048,4096]{1,0:T(8,128)(2,1)} %wq_hbm.1, bf16[2048,512]{1,0:T(8,128)(2,1)} %wk_hbm.1, bf16[2048,512]{1,0:T(8,128)(2,1)} %wv_hbm.1, bf16[4096,2048]{1,0:T(8,128)(2,1)} %wo_hbm.1, s32[2,16]{1,0:T(2,128)} %bitcast.1, ...), custom_call_target="tpu_custom_call" | custom-call | tf_op jit(solution)/shard_map/attention_block/pallas_call | solution.py:445
  35.8 3.4 %store_outputs.1 = (bf16[4,512,2048]{2,1,0:T(8,128)(2,1)}, bf16[16,2048]{1,0:T(8,128)(2,1)}) custom-call(bf16[4,512,2048]{2,1,0:T(8,128)(2,1)S(1)} %get-tuple-element.6.buf_ref, bf16[16,2048]{1,0:T(8,128)(2,1)S(1)} %get-tuple-element.7.h_ref), custom_call_target="tpu_custom_call" | custom-call | tf_op jit(solution)/shard_map/store_outputs/pallas_call | solution.py:479

commit v6 on v5

--- a/solution.py
+++ b/solution.py
@@ -20,10 +20,28 @@
 BF16 = jnp.bfloat16
 
 
+def group_rows(side, tok2, half, g, a):
+    slot = (g + (a - g) * half) * side + a + (g - a) * half
+    return pl.ds(pl.multiple_of(slot * tok2, tok2), tok2)
+
+
+def build_group(side, tok2, n_exp, h_ref, sel_ref, gate_ref, half, g, put):
+    g_tok = side * tok2
+    n = half * side + g
+    for q in range(h_ref.shape[3] // B_COLS):
+        h_g = h_ref[half, pl.ds(g * side, side), :, q * B_COLS:(q + 1) * B_COLS].reshape(g_tok, B_COLS)
+        rows = jnp.dot(sel_ref[n], h_g, preferred_element_type=F32)
+        gate = gate_ref[n]
+        rows = jnp.concatenate([rows[:, i * LANES:(i + 1) * LANES] * gate for i in range(B_COLS // LANES)], axis=1)
+        rows = rows.astype(BF16)
+        for a in range(side):
+            for k in range(n_exp):
+                put(a, k, q, rows[k * g_tok + a * tok2:k * g_tok + (a + 1) * tok2, :])
+
+
 def block_kernel(side, x_hbm, wq_hbm, wk_hbm, wv_hbm, wo_hbm, ids_hbm, probs_hbm,
-                 buf_out, h_out,
+                 buf_out, h_buf, sel_s, gate_s,
                  xbuf, wq_v, wk_v, wv_v, wo_v, ids_v, probs_v, kv_own, kvbuf, meta_own, meta_buf, q_s, o_own, o_sib,
-                 h_buf, sel_s, gate_s,
                  wsem, pair_send, pair_recv, kv_send, kv_recv, kv2_send, kv2_recv, mt_send, mt_recv, h_send, h_recv,
                  d_send, d_recv):
     tok = x_hbm.shape[0]
@@ -341,19 +359,11 @@
     lax.fori_loop(0, side, select_rows, 0)
 
     def build(half, g):
-        n = half * side + g
-        for q in range(half_w // B_COLS):
-            h_g = h_buf[half, pl.ds(g * side, side), :, q * B_COLS:(q + 1) * B_COLS].reshape(g_tok, B_COLS)
-            rows = jnp.dot(sel_s[n], h_g, preferred_element_type=F32)
-            gate = gate_s[n]
-            rows = jnp.concatenate([rows[:, i * LANES:(i + 1) * LANES] * gate for i in range(B_COLS // LANES)], axis=1)
-            rows = rows.astype(BF16)
+        def put(a, k, q, rows):
             cols = pl.ds(pl.multiple_of(half * half_w + q * B_COLS, B_COLS), B_COLS)
-            for a in range(side):
-                slot = (g + (a - g) * half) * side + a + (g - a) * half
-                at = pl.ds(pl.multiple_of(slot * tok2, tok2), tok2)
-                for k in range(own_experts):
-                    buf_out[k, at, cols] = rows[k * g_tok + a * tok2:k * g_tok + (a + 1) * tok2, :]
+            buf_out[k, group_rows(side, tok2, half, g, a), cols] = rows
+
+        build_group(side, tok2, own_experts, h_buf, sel_s, gate_s, half, g, put)
 
     def take_first(k):
         i = back(a0, k)
@@ -368,34 +378,35 @@
             hg.relay(i, relays[k]).start()
         cross(i, j).start()
 
+    def other_done(d):
+        for a in range(side):
+            cross_from(back(a0, d) * side + a).wait_recv()
+
     def build_other(d):
-        g = back(a0, d)
-        for a in range(side):
-            cross_from(g * side + a).wait_recv()
-        build(1 - core, g)
+        other_done(d)
+        build(1 - core, back(a0, d))
 
     take_first(1)
     take_first(side - 1)
     take(0, 1)
     take_first(2)
     build(core, b0)
+    build_other(0)
     take(1, side - 1)
     take(side - 1, side - 1)
     for k in (1, side - 1, 2):
         take(k, 1)
-    build(core, back(b0, 1))
-    build_other(0)
     take(0, side - 1)
     take(2, side - 1)
+    for k in (0, 2):
+        take(k, 2)
+    build(core, back(b0, 1))
+    build_other(1)
     build(core, back(b0, side - 1))
-    build_other(1)
-    for k in (0, 2, 1, side - 1):
+    for k in (1, side - 1):
         take(k, 2)
-    build_other(side - 1)
-    build(core, back(b0, 2))
-    build_other(2)
-    for c in range(CORES):
-        h_out[:, c * half_w:(c + 1) * half_w] = h_buf[c, cx * side + cy if c else chip, my_rows, :]
+    for d in (side - 1, 2):
+        other_done(d)
 
     for c in [x_pair, m_pair, kv_pair] + o_pairs:
         c.wait_send()
@@ -411,12 +422,44 @@
             cross(i, j).wait_send()
 
 
-def store_kernel(buf_ref, h_ref, buf_out, h_out, sem):
-    n = buf_ref.shape[0]
-    copies = [pltpu.make_async_copy(buf_ref.at[k], buf_out.at[k], sem.at[k]) for k in range(n)]
-    copies.append(pltpu.make_async_copy(h_ref, h_out, sem.at[n]))
-    for c in copies:
-        c.start()
+def store_kernel(side, buf_ref, h_ref, sel_ref, gate_ref, buf_out, h_out, stage, sem, stage_sem, h_sem):
+    n_exp = buf_ref.shape[0]
+    tok2, half_w = h_ref.shape[2:]
+    tok = h_out.shape[0]
+    me = lax.axis_index('sp')
+    core = me % CORES
+    chip = me // CORES
+    cy = chip // side
+    cx = chip % side
+    a0 = cx + (cy - cx) * core
+    b0 = cy + (cx - cy) * core
+    copies = []
+
+    def start(src, dst, s):
+        copies.append(pltpu.make_async_copy(src, dst, s))
+        copies[-1].start()
+
+    def cols(half):
+        return pl.ds(pl.multiple_of(half * half_w, half_w), half_w)
+
+    other = 1 - core
+    done = [(core, b0), (core, (b0 - 1 + side) % side), (core, (b0 + 1) % side), (other, a0), (other, (a0 - 1 + side) % side)]
+    for n, (half, g) in enumerate(done):
+        for a in range(side):
+            rows = group_rows(side, tok2, half, g, a)
+            start(buf_ref.at[:, rows, cols(half)], buf_out.at[:, rows, cols(half)], sem.at[n * side + a])
+    my_rows = pl.ds(pl.multiple_of(core * tok, tok), tok)
+    for c in range(CORES):
+        start(h_ref.at[c, cx * side + cy if c else chip, my_rows, :], h_out.at[:, pl.ds(c * half_w, half_w)], h_sem.at[c])
+    rest = [(core, (b0 + 2) % side), (other, (a0 + 1) % side), (other, (a0 + 2) % side)]
+    for n, (half, g) in enumerate(rest):
+        def put(a, k, q, rows, n=n):
+            stage[n, k, a * tok2:(a + 1) * tok2, q * B_COLS:(q + 1) * B_COLS] = rows
+
+        build_group(side, tok2, n_exp, h_ref, sel_ref, gate_ref, half, g, put)
+        for a in range(side):
+            start(stage.at[n, :, pl.ds(a * tok2, tok2), :], buf_out.at[:, group_rows(side, tok2, half, g, a), cols(half)],
+                  stage_sem.at[n * side + a])
     for c in copies:
         c.wait()
 
@@ -442,11 +485,15 @@
         dma = pltpu.SemaphoreType.DMA
         n_loads = 7 + half_q // Q_COLS
         kv_half_heads = half_kv // HEAD_DIM
-        buf, h = pl.pallas_call(
+        g_tok = side * tok2
+        parts = pl.pallas_call(
             functools.partial(block_kernel, side),
-            out_shape=(pltpu.VMEM((own, tok * group, width), BF16), pltpu.VMEM((tok, width), BF16)),
+            out_shape=(pltpu.VMEM((own, tok * group, width), BF16),
+                       pltpu.VMEM((CORES, chips, tok2, half_w), BF16),
+                       pltpu.VMEM((CORES * side, own * g_tok, g_tok), BF16),
+                       pltpu.VMEM((CORES * side, own * g_tok, LANES), F32)),
             in_specs=[hbm_spec] * 7,
-            out_specs=(vmem_spec, vmem_spec),
+            out_specs=(vmem_spec,) * 4,
             scratch_shapes=[
                 pltpu.VMEM((tok2, width), BF16),
                 pltpu.VMEM((width, half_q), BF16),
@@ -462,9 +509,6 @@
                 pltpu.VMEM((tok2, half_q), BF16),
                 pltpu.VMEM((tok2, half_q), BF16),
                 pltpu.VMEM((tok2, half_q), BF16),
-                pltpu.VMEM((CORES, chips, tok2, half_w), BF16),
-                pltpu.VMEM((CORES * side, own * side * tok2, side * tok2), BF16),
-                pltpu.VMEM((CORES * side, own * side * tok2, LANES), F32),
                 dma((n_loads,)),
                 dma((3 + kv_half_heads,)), dma((3 + kv_half_heads,)),
                 dma((CORES * side,)), dma((CORES * side,)),
@@ -473,18 +517,19 @@
                 dma((chips,)), dma((chips,)),
             ],
             compiler_params=pltpu.CompilerParams(collective_id=0, has_side_effects=True,
-                                                 vmem_limit_bytes=55 * 2 ** 20 + 850 * 1024),
+                                                 vmem_limit_bytes=50 * 2 ** 20 + 900 * 1024),
             name='attention_block',
         )(x_loc, w_q, w_k, w_v, w_o, ids_loc.T, probs_loc)
         buf, h = pl.pallas_call(
-            store_kernel,
+            functools.partial(store_kernel, side),
             out_shape=(jax.ShapeDtypeStruct((own, tok * group, width), BF16), jax.ShapeDtypeStruct((tok, width), BF16)),
-            in_specs=[vmem_spec, vmem_spec],
+            in_specs=[vmem_spec] * 4,
             out_specs=(any_spec, any_spec),
-            scratch_shapes=[dma((own + 1,))],
+            scratch_shapes=[pltpu.VMEM((3, own, g_tok, half_w), BF16),
+                            dma((5 * side,)), dma((3 * side,)), dma((CORES,))],
             compiler_params=pltpu.CompilerParams(vmem_limit_bytes=16 * 2 ** 20),
             name='store_outputs',
-        )(buf, h)
+        )(*parts)
         return h, buf
 
     return jax.shard_map(device_step, mesh=mesh, in_specs=(row_spec, P(), P(), P(), P(), row_spec, row_spec), out_specs=(row_spec, buf_spec), check_vma=False)

time: 39.3 us -> 38.5 us (0.980)
  Pallas kernels: 38.6 us -> 37.8 us
    pallas_call x1, Pallas kernels: 35.2 us -> 34.2 us  [device_step(): pl.pallas_call(functools.partial(block_kernel, side), out_shape=(pltpu.VM...]
where the time goes in v6:
time: 38.5 us
  Pallas kernels  37.8 us (98%)
  between operations  0.64 us (2%)
    pallas_call x1, Pallas kernels, device_step(): pl.pallas_call(functools.partial(block_kernel, side), out_shape=(pltpu.VM...  34.2 us
    pallas_call x1, Pallas kernels, device_step(): pl.pallas_call(functools.partial(store_kernel, side), out_shape=(jax.Shap...  3.61 us

profile of v6, /device:TPU:97, one launch (start us, length us, event | category | flops | bytes accessed | tf_op | source)
XLA Modules:
  0.0 38.5 jit_solution(9758245946502505708)
XLA Ops:
  0.6 34.2 %attention_block.1 = (bf16[4,512,2048]{2,1,0:T(8,128)(2,1)S(1)}, bf16[2,16,32,1024]{3,2,1,0:T(8,128)(2,1)S(1)}, bf16[8,512,128]{2,1,0:T(8,128)(2,1)S(1)}, f32[8,512,128]{2,1,0:T(8,128)S(1)}) custom-call(bf16[16,2048]{1,0:T(8,128)(2,1)} %x_hbm.1, bf16[2048,4096]{1,0:T(8,128)(2,1)} %wq_hbm.1, bf16[2048,512]{1,0:T(8,128)(2,1)} %wk_hbm.1, ...), custom_call_target="tpu_custom_call" | custom-call | tf_op jit(solution)/shard_map/attention_block/pallas_call | solution.py:489
  34.9 3.6 %store_outputs.1 = (bf16[4,512,2048]{2,1,0:T(8,128)(2,1)}, bf16[16,2048]{1,0:T(8,128)(2,1)}) custom-call(bf16[4,512,2048]{2,1,0:T(8,128)(2,1)S(1)} %get-tuple-element.8.buf_ref, bf16[2,16,32,1024]{3,2,1,0:T(8,128)(2,1)S(1)} %get-tuple-element.9.h_ref, bf16[8,512,128]{2,1,0:T(8,128)(2,1)S(1)} %get-tuple-element.10.sel_ref, ...), custom_call_target="tpu_custom_call" | custom-call | tf_op jit(solution)/shard_map/store_outputs/pallas_call | solution.py:523

commit v7 on v6

--- a/solution.py
+++ b/solution.py
@@ -78,6 +78,18 @@
         return pltpu.make_async_remote_copy(src_ref=src, dst_ref=dst, send_sem=ss, recv_sem=rs,
                                             device_id=dev, device_id_type=MESH_IDS)
 
+    my_rows = pl.ds(pl.multiple_of(core * tok, tok), tok)
+    loads = {}
+
+    def load(name, src, dst):
+        loads[name] = pltpu.make_async_copy(src, dst, wsem.at[len(loads)])
+        loads[name].start()
+
+    load('x', x_hbm, xbuf.at[my_rows, :])
+    load('ids', ids_hbm, ids_v)
+    load('probs', probs_hbm, probs_v)
+    load('k', wk_hbm, wk_v)
+    load('v', wv_hbm, wv_v)
     barrier = pltpu.get_barrier_semaphore()
     partners = [sib]
     for d in range(1, side):
@@ -87,18 +99,6 @@
     for p in partners:
         pl.semaphore_signal(barrier, inc=1, device_id=p, device_id_type=MESH_IDS)
 
-    my_rows = pl.ds(pl.multiple_of(core * tok, tok), tok)
-    loads = {}
-
-    def load(name, src, dst):
-        loads[name] = pltpu.make_async_copy(src, dst, wsem.at[len(loads)])
-        loads[name].start()
-
-    load('x', x_hbm, xbuf.at[my_rows, :])
-    load('ids', ids_hbm, ids_v)
-    load('probs', probs_hbm, probs_v)
-    load('k', wk_hbm, wk_v)
-    load('v', wv_hbm, wv_v)
     n_q = half_q // Q_COLS
     for i in range(n_q):
         load(('q', i), wq_hbm.at[:, pl.ds(pl.multiple_of(core * half_q + i * Q_COLS, Q_COLS), Q_COLS)],

time: 38.5 us -> 38.2 us (level)
  no operation moved by 1% of the time
where the time goes in v7:
time: 38.2 us; the launch traced here: 38.1 us
  Pallas kernels  37.5 us (98%)
  between operations  0.64 us (2%)
    pallas_call x1, Pallas kernels, device_step(): pl.pallas_call(functools.partial(block_kernel, side), out_shape=(pltpu.VM...  33.9 us
    pallas_call x1, Pallas kernels, device_step(): pl.pallas_call(functools.partial(store_kernel, side), out_shape=(jax.Shap...  3.61 us

profile of v7, /device:TPU:97, one launch (start us, length us, event | category | flops | bytes accessed | tf_op | source)
XLA Modules:
  0.0 38.1 jit_solution(7770107946426863638)
XLA Ops:
  0.6 33.9 %attention_block.1 = (bf16[4,512,2048]{2,1,0:T(8,128)(2,1)S(1)}, bf16[2,16,32,1024]{3,2,1,0:T(8,128)(2,1)S(1)}, bf16[8,512,128]{2,1,0:T(8,128)(2,1)S(1)}, f32[8,512,128]{2,1,0:T(8,128)S(1)}) custom-call(bf16[16,2048]{1,0:T(8,128)(2,1)} %x_hbm.1, bf16[2048,4096]{1,0:T(8,128)(2,1)} %wq_hbm.1, bf16[2048,512]{1,0:T(8,128)(2,1)} %wk_hbm.1, ...), custom_call_target="tpu_custom_call" | custom-call | tf_op jit(solution)/shard_map/attention_block/pallas_call | solution.py:489
  34.5 3.6 %store_outputs.1 = (bf16[4,512,2048]{2,1,0:T(8,128)(2,1)}, bf16[16,2048]{1,0:T(8,128)(2,1)}) custom-call(bf16[4,512,2048]{2,1,0:T(8,128)(2,1)S(1)} %get-tuple-element.8.buf_ref, bf16[2,16,32,1024]{3,2,1,0:T(8,128)(2,1)S(1)} %get-tuple-element.9.h_ref, bf16[8,512,128]{2,1,0:T(8,128)(2,1)S(1)} %get-tuple-element.10.sel_ref, ...), custom_call_target="tpu_custom_call" | custom-call | tf_op jit(solution)/shard_map/store_outputs/pallas_call | solution.py:523

commit v8 on v7

--- a/solution.py
+++ b/solution.py
@@ -163,7 +163,7 @@
         return remote(kv_own.at[c], kvbuf.at[chip_at(i, b0), pl.ds(c * tok, tok), :], kv_send.at[0],
                       kv_recv.at[CORES * i + c], sib)
 
-    for d in (2, 1, side - 1):
+    for d in (1, side - 1, 2):
         for c in range(CORES):
             kv_first(d, c).start()
 
@@ -235,19 +235,18 @@
     x_pair.wait_recv()
     project_q(range(Q_EARLY))
 
-    def kv_pass(i, carry):
-        @pl.when(i != a0)
-        def _():
-            for c in range(CORES):
-                kv_first_from(i, c).wait_recv()
-            kv_second(i, False)
-            mt.first_from(i).wait_recv()
-            mt.spread(i)
-        return carry
-
-    lax.fori_loop(0, side, kv_pass, 0)
+    for d in (1, side - 1, 2):
+        i = (a0 - d + side) % side
+        for c in range(CORES):
+            kv_first_from(i, c).wait_recv()
+        kv_second(i, False)
 
     project_q(range(Q_EARLY, n_q))
+
+    for d in (1, side - 1, 2):
+        i = (a0 - d + side) % side
+        mt.first_from(i).wait_recv()
+        mt.spread(i)
 
     def kv_done(n, carry):
         i, j = n // side, n % side

time: 38.2 us -> 38.1 us (level)
  no operation moved by 1% of the time
where the time goes in v8:
time: 38.1 us; the launch traced here: 38 us
  Pallas kernels  37.3 us (98%)
  between operations  0.64 us (2%)
    pallas_call x1, Pallas kernels, device_step(): pl.pallas_call(functools.partial(block_kernel, side), out_shape=(pltpu.VM...  33.7 us
    pallas_call x1, Pallas kernels, device_step(): pl.pallas_call(functools.partial(store_kernel, side), out_shape=(jax.Shap...  3.61 us

profile of v8, /device:TPU:97, one launch (start us, length us, event | category | flops | bytes accessed | tf_op | source)
XLA Modules:
  0.0 38.0 jit_solution(12672434936481143804)
XLA Ops:
  0.6 33.7 %attention_block.1 = (bf16[4,512,2048]{2,1,0:T(8,128)(2,1)S(1)}, bf16[2,16,32,1024]{3,2,1,0:T(8,128)(2,1)S(1)}, bf16[8,512,128]{2,1,0:T(8,128)(2,1)S(1)}, f32[8,512,128]{2,1,0:T(8,128)S(1)}) custom-call(bf16[16,2048]{1,0:T(8,128)(2,1)} %x_hbm.1, bf16[2048,4096]{1,0:T(8,128)(2,1)} %wq_hbm.1, bf16[2048,512]{1,0:T(8,128)(2,1)} %wk_hbm.1, ...), custom_call_target="tpu_custom_call" | custom-call | tf_op jit(solution)/shard_map/attention_block/pallas_call | solution.py:488
  34.4 3.6 %store_outputs.1 = (bf16[4,512,2048]{2,1,0:T(8,128)(2,1)}, bf16[16,2048]{1,0:T(8,128)(2,1)}) custom-call(bf16[4,512,2048]{2,1,0:T(8,128)(2,1)S(1)} %get-tuple-element.8.buf_ref, bf16[2,16,32,1024]{3,2,1,0:T(8,128)(2,1)S(1)} %get-tuple-element.9.h_ref, bf16[8,512,128]{2,1,0:T(8,128)(2,1)S(1)} %get-tuple-element.10.sel_ref, ...), custom_call_target="tpu_custom_call" | custom-call | tf_op jit(solution)/shard_map/store_outputs/pallas_call | solution.py:522

commit v9 on v8

--- a/solution.py
+++ b/solution.py
@@ -400,11 +400,9 @@
     for k in (0, 2):
         take(k, 2)
     build(core, back(b0, 1))
-    build_other(1)
-    build(core, back(b0, side - 1))
     for k in (1, side - 1):
         take(k, 2)
-    for d in (side - 1, 2):
+    for d in (1, side - 1, 2):
         other_done(d)
 
     for c in [x_pair, m_pair, kv_pair] + o_pairs:
@@ -442,7 +440,7 @@
         return pl.ds(pl.multiple_of(half * half_w, half_w), half_w)
 
     other = 1 - core
-    done = [(core, b0), (core, (b0 - 1 + side) % side), (core, (b0 + 1) % side), (other, a0), (other, (a0 - 1 + side) % side)]
+    done = [(core, b0), (core, (b0 - 1 + side) % side), (other, a0)]
     for n, (half, g) in enumerate(done):
         for a in range(side):
             rows = group_rows(side, tok2, half, g, a)
@@ -450,7 +448,7 @@
     my_rows = pl.ds(pl.multiple_of(core * tok, tok), tok)
     for c in range(CORES):
         start(h_ref.at[c, cx * side + cy if c else chip, my_rows, :], h_out.at[:, pl.ds(c * half_w, half_w)], h_sem.at[c])
-    rest = [(core, (b0 + 2) % side), (other, (a0 + 1) % side), (other, (a0 + 2) % side)]
+    rest = [(other, (a0 - 1 + side) % side), (core, (b0 + 1) % side), (core, (b0 + 2) % side), (other, (a0 + 1) % side), (other, (a0 + 2) % side)]
     for n, (half, g) in enumerate(rest):
         def put(a, k, q, rows, n=n):
             stage[n, k, a * tok2:(a + 1) * tok2, q * B_COLS:(q + 1) * B_COLS] = rows
@@ -524,8 +522,8 @@
             out_shape=(jax.ShapeDtypeStruct((own, tok * group, width), BF16), jax.ShapeDtypeStruct((tok, width), BF16)),
             in_specs=[vmem_spec] * 4,
             out_specs=(any_spec, any_spec),
-            scratch_shapes=[pltpu.VMEM((3, own, g_tok, half_w), BF16),
-                            dma((5 * side,)), dma((3 * side,)), dma((CORES,))],
+            scratch_shapes=[pltpu.VMEM((5, own, g_tok, half_w), BF16),
+                            dma((3 * side,)), dma((5 * side,)), dma((CORES,))],
             compiler_params=pltpu.CompilerParams(vmem_limit_bytes=16 * 2 ** 20),
             name='store_outputs',
         )(*parts)

time: 38.1 us -> 36.9 us (0.969)
  Pallas kernels: 37.3 us -> 36.2 us
    pallas_call x1, Pallas kernels: 33.7 us -> 32.6 us  [device_step(): pl.pallas_call(functools.partial(block_kernel, side), out_shape=(pltpu.VM...]
where the time goes in v9:
time: 36.9 us; the launch traced here: 36.8 us
  Pallas kernels  36.2 us (98%)
  between operations  0.64 us (2%)
    pallas_call x1, Pallas kernels, device_step(): pl.pallas_call(functools.partial(block_kernel, side), out_shape=(pltpu.VM...  32.6 us
    pallas_call x1, Pallas kernels, device_step(): pl.pallas_call(functools.partial(store_kernel, side), out_shape=(jax.Shap...  3.61 us

profile of v9, /device:TPU:97, one launch (start us, length us, event | category | flops | bytes accessed | tf_op | source)
XLA Modules:
  0.0 36.8 jit_solution(15173158842152672314)
XLA Ops:
  0.6 32.6 %attention_block.1 = (bf16[4,512,2048]{2,1,0:T(8,128)(2,1)S(1)}, bf16[2,16,32,1024]{3,2,1,0:T(8,128)(2,1)S(1)}, bf16[8,512,128]{2,1,0:T(8,128)(2,1)S(1)}, f32[8,512,128]{2,1,0:T(8,128)S(1)}) custom-call(bf16[16,2048]{1,0:T(8,128)(2,1)} %x_hbm.1, bf16[2048,4096]{1,0:T(8,128)(2,1)} %wq_hbm.1, bf16[2048,512]{1,0:T(8,128)(2,1)} %wk_hbm.1, ...), custom_call_target="tpu_custom_call" | custom-call | tf_op jit(solution)/shard_map/attention_block/pallas_call | solution.py:486
  33.2 3.6 %store_outputs.1 = (bf16[4,512,2048]{2,1,0:T(8,128)(2,1)}, bf16[16,2048]{1,0:T(8,128)(2,1)}) custom-call(bf16[4,512,2048]{2,1,0:T(8,128)(2,1)S(1)} %get-tuple-element.8.buf_ref, bf16[2,16,32,1024]{3,2,1,0:T(8,128)(2,1)S(1)} %get-tuple-element.9.h_ref, bf16[8,512,128]{2,1,0:T(8,128)(2,1)S(1)} %get-tuple-element.10.sel_ref, ...), custom_call_target="tpu_custom_call" | custom-call | tf_op jit(solution)/shard_map/store_outputs/pallas_call | solution.py:520

commit v10 on v9

--- a/solution.py
+++ b/solution.py
@@ -145,27 +145,27 @@
     kvbuf[chip, my_rows, :] = kv_own[core]
 
     pl.semaphore_wait(barrier, len(partners))
+    def kv_first(d, c):
+        y = (cy + d * c) % side
+        x = (cx + d * (1 - c)) % side
+        i = cx + (cy - cx) * c
+        return remote(kv_own.at[c], kvbuf.at[chip, my_rows, :], kv_send.at[CORES * d + c],
+                      kv_recv.at[CORES * i + core], {'sp': (y * side + x) * CORES + c})
+
+    def kv_first_from(i, c):
+        return remote(kv_own.at[c], kvbuf.at[chip_at(i, b0), pl.ds(c * tok, tok), :], kv_send.at[0],
+                      kv_recv.at[CORES * i + c], sib)
+
+    for d in (1, side - 1, 2):
+        for c in range(CORES):
+            kv_first(d, c).start()
+
     x_pair = remote(xbuf.at[my_rows, :], xbuf.at[my_rows, :], pair_send.at[0], pair_recv.at[0], sib)
     x_pair.start()
     m_pair = remote(meta_own.at[0], meta_own.at[1], pair_send.at[1], pair_recv.at[1], sib)
     m_pair.start()
     kv_pair = remote(kv_own.at[1 - core], kvbuf.at[chip, my_rows, :], pair_send.at[2], pair_recv.at[2], sib)
     kv_pair.start()
-
-    def kv_first(d, c):
-        y = (cy + d * c) % side
-        x = (cx + d * (1 - c)) % side
-        i = cx + (cy - cx) * c
-        return remote(kv_own.at[c], kvbuf.at[chip, my_rows, :], kv_send.at[CORES * d + c],
-                      kv_recv.at[CORES * i + core], {'sp': (y * side + x) * CORES + c})
-
-    def kv_first_from(i, c):
-        return remote(kv_own.at[c], kvbuf.at[chip_at(i, b0), pl.ds(c * tok, tok), :], kv_send.at[0],
-                      kv_recv.at[CORES * i + c], sib)
-
-    for d in (1, side - 1, 2):
-        for c in range(CORES):
-            kv_first(d, c).start()
 
     class Gather:
         def __init__(self, ref, ss, rs):
@@ -390,9 +390,9 @@
     take(0, 1)
     take_first(2)
     build(core, b0)
-    build_other(0)
     take(1, side - 1)
     take(side - 1, side - 1)
+    build_other(0)
     for k in (1, side - 1, 2):
         take(k, 1)
     take(0, side - 1)

time: 36.9 us -> 36.9 us (level)
  no operation moved by 1% of the time
where the time goes in v10:
time: 36.9 us; the launch traced here: 36.8 us
  Pallas kernels  36.2 us (98%)
  between operations  0.64 us (2%)
    pallas_call x1, Pallas kernels, device_step(): pl.pallas_call(functools.partial(block_kernel, side), out_shape=(pltpu.VM...  32.6 us
    pallas_call x1, Pallas kernels, device_step(): pl.pallas_call(functools.partial(store_kernel, side), out_shape=(jax.Shap...  3.61 us

profile of v10, /device:TPU:97, one launch (start us, length us, event | category | flops | bytes accessed | tf_op | source)
XLA Modules:
  0.0 36.8 jit_solution(15503897400527624637)
XLA Ops:
  0.6 32.6 %attention_block.1 = (bf16[4,512,2048]{2,1,0:T(8,128)(2,1)S(1)}, bf16[2,16,32,1024]{3,2,1,0:T(8,128)(2,1)S(1)}, bf16[8,512,128]{2,1,0:T(8,128)(2,1)S(1)}, f32[8,512,128]{2,1,0:T(8,128)S(1)}) custom-call(bf16[16,2048]{1,0:T(8,128)(2,1)} %x_hbm.1, bf16[2048,4096]{1,0:T(8,128)(2,1)} %wq_hbm.1, bf16[2048,512]{1,0:T(8,128)(2,1)} %wk_hbm.1, ...), custom_call_target="tpu_custom_call" | custom-call | tf_op jit(solution)/shard_map/attention_block/pallas_call | solution.py:486
  33.2 3.6 %store_outputs.1 = (bf16[4,512,2048]{2,1,0:T(8,128)(2,1)}, bf16[16,2048]{1,0:T(8,128)(2,1)}) custom-call(bf16[4,512,2048]{2,1,0:T(8,128)(2,1)S(1)} %get-tuple-element.8.buf_ref, bf16[2,16,32,1024]{3,2,1,0:T(8,128)(2,1)S(1)} %get-tuple-element.9.h_ref, bf16[8,512,128]{2,1,0:T(8,128)(2,1)S(1)} %get-tuple-element.10.sel_ref, ...), custom_call_target="tpu_custom_call" | custom-call | tf_op jit(solution)/shard_map/store_outputs/pallas_call | solution.py:520
